TPU v7x, 32 devices: a whole 2x2x4 slice. The times are simulated.
32 devices in a mesh: band: 8 (over z, x), img: 4 (over y, core).
Axes of the slice: x: 2, y: 2, z: 4, core: 2. Of those that a mesh axis runs over, the one named last changes fastest.
Arguments:
- pixels: bfloat16 [256, 256, 180], P(('img', 'band')), parts along dimension 0, may hold values from -12 to 12
- keep_mask: int32 [32, 32], P(('img', 'band')), parts along dimension 0, may hold values from 0 to 1, as said below
- band_counts: int32 [32], P(('img', 'band')), parts along dimension 0, may hold values from 0 to 32, as said below
- plan_dest: int32 [32, 16], P(('img', 'band')), parts along dimension 0, may hold values from 0 to 7, as said below
- plan_slot: int32 [32, 16], P(('img', 'band')), parts along dimension 0, may hold values from 0 to 8, as said below
- bias_table: float32 [225, 6], replicated, may hold values from -4 to 4
- gain_attn: float32 [180], replicated, may hold values from 0.25 to 1.75
- qkv_weight: bfloat16 [180, 540], replicated, may hold values from -5 to 5
- proj_weight: bfloat16 [180, 180], replicated, may hold values from -0.4375 to 0.4375
- gain_mlp: float32 [180], replicated, may hold values from 0.25 to 1.75
- hidden_weight: bfloat16 [180, 360], replicated, may hold values from -0.4375 to 0.4375
- output_weight: bfloat16 [360, 180], replicated, may hold values from -0.3125 to 0.3125
Outputs:
- restored: bfloat16 [256, 256, 180], P(('img', 'band')), parts along dimension 0
- work_tiles: bfloat16 [256, 128, 180], P(('img', 'band')), parts along dimension 0
There are 4 independent parts, one for each index of `img`. A program takes and returns all parts, laid end to end along the dimension named above; an argument that names none is the same for every part. Nothing has to cross between parts.
Inputs may be any that keep to these rules, and one draw needn't show every extreme that they name: `keep_mask`: the number of ones in a band varies strongly from band to band. band_counts[b] equals the number of ones among band b's windows in keep_mask. A band's live tiles are those with 2 t < band_counts[b]; their number summed over bands lies between 57 and 64, and some band has all 16 tiles live. `plan_dest`: within each aligned group of 8 consecutive tiles of a band (equal t // 8) the destinations are all different. `plan_slot`: 8 for tiles that are not live; a live tile has a slot below 8, no two live tiles of the image share destination and slot, and some destination receives 8 live tiles.
All inputs are finite; a program needn't handle non-finite values.
Results may differ from a plain program's by a relative error of at most 0.0044.
Values may be sent and summed in bfloat16 or wider, within the bound.
A program may use at most 64 MiB of HBM per device.

v0:
```python
import jax
import jax.numpy as jnp
from jax import lax
from jax.experimental import pallas as pl
from jax.experimental.pallas import tpu as pltpu
from jax.sharding import PartitionSpec as P

CHAN = 180
HEADS = 6
WIN = 8
TILE = 2
SHIFT = 4
CAP = 8
TOK = WIN * WIN
HALF = TOK // 2
HEAD_DIM = CHAN // HEADS
GROUP = 4
LANES = 128
SLOT_LANE = 120

EPSILON = 1e-05
BF = jnp.bfloat16
F32 = jnp.float32


def layer_norm(values, gain_vec):
    center = values - jnp.sum(values, axis=-1, keepdims=True) * (1.0 / CHAN)
    spread = jnp.sum(center * center, axis=-1, keepdims=True) * (1.0 / CHAN)
    return (center * lax.rsqrt(spread + EPSILON) * gain_vec).astype(BF)


def dot(a, b):
    return jnp.dot(a, b, preferred_element_type=F32)


def dot_t(a, b):
    return lax.dot_general(a, b, (((1,), (1,)), ((), ())), preferred_element_type=F32)


def biases(bias_ref, last_row, queries):
    first = TOK - queries
    base = jnp.concatenate([bias_ref[h][first:] for h in range(HEADS)], axis=0)
    shape = (HEADS * queries, TOK)
    key = lax.broadcasted_iota(jnp.int32, shape, 1)
    query = lax.broadcasted_iota(jnp.int32, shape, 0) % queries + first
    rows_differ = (key // WIN >= SHIFT) != (query // WIN >= SHIFT)
    cols_differ = (key % WIN >= SHIFT) != (query % WIN >= SHIFT)
    row_pen = jnp.where(rows_differ, jnp.where(last_row, -100.0, 0.0).astype(F32), 0.0)
    plain = base + row_pen
    both = base + jnp.where(cols_differ, -100.0, row_pen)
    return plain, both


def head_masks():
    lane = lax.broadcasted_iota(jnp.int32, (1, CHAN), 1)
    return [
        ((lane >= h * HEAD_DIM) & (lane < (h + 1) * HEAD_DIM)).astype(F32) for h in range(HEADS)
    ]


def attend(x, gain, wq, wk, wv, wp, bias_of, queries):
    masks = head_masks()
    low_masks = [m.astype(BF) for m in masks]
    normed = layer_norm(x, gain)
    if queries == TOK:
        x_q, n_q = x, normed
    else:
        pick = lambda a: jnp.concatenate(
            [a[g * TOK + TOK - queries : (g + 1) * TOK] for g in range(GROUP)], axis=0
        )
        x_q, n_q = pick(x), pick(normed)
    q = (dot(n_q, wq) * HEAD_DIM ** (-0.5)).astype(BF)
    k = dot(normed, wk).astype(BF)
    v = dot(normed, wv).astype(BF)
    mixed = []
    for g in range(GROUP):
        q_w = q[g * queries : (g + 1) * queries]
        stacked = jnp.concatenate([q_w * low_masks[h] for h in range(HEADS)], axis=0)
        scores = dot_t(stacked, k[g * TOK : (g + 1) * TOK]) + bias_of(g)
        top = jnp.max(scores, axis=1, keepdims=True)
        grown = jnp.exp(scores - top)
        weights = (grown * (1.0 / jnp.sum(grown, axis=1, keepdims=True))).astype(BF)
        wide = dot(weights, v[g * TOK : (g + 1) * TOK])
        total = wide[:queries] * masks[0]
        for h in range(1, HEADS):
            total = total + wide[h * queries : (h + 1) * queries] * masks[h]
        mixed.append(total)
    mixed = jnp.concatenate(mixed, axis=0).astype(BF)
    return (x_q + dot(mixed, wp)).astype(BF)


def feed(states, gain, wh, wo):
    flat = states.astype(F32)
    normed = layer_norm(flat, gain)
    inner = jax.nn.gelu(dot(normed, wh)).astype(BF)
    return (flat + dot_t(inner, wo)).astype(BF)


def roll_cols(x, by):
    by = by % x.shape[1]
    return jnp.concatenate([x[:, by:], x[:, :by]], axis=1)


def window_at(shifted, i, g, row):
    start = pl.multiple_of((i * GROUP + g) * WIN, WIN)
    return shifted[row : row + WIN, pl.ds(start, WIN), :].reshape(TOK, CHAN)


def group_at(shifted, i):
    return jnp.concatenate([window_at(shifted, i, g, 0) for g in range(GROUP)], axis=0)


def own_kernel(
    pixels, told, bias, gain_a, wq, wk, wv, wp,
    upper, first, rest, prv, facts,
    shifted, nxt_buf, prv_buf, facts_buf, bias_own, send_sem, recv_sem,
):
    bands = lax.axis_size("band")
    me = lax.axis_index("band")
    right, left = lax.rem(me + 1, bands), lax.rem(me + bands - 1, bands)
    rows, cols, _ = pixels.shape
    windows = cols // WIN
    groups = windows // GROUP
    chunks = groups // 2
    width = cols // chunks

    barrier = pltpu.get_barrier_semaphore()
    for neighbour in (left, right):
        pl.semaphore_signal(
            barrier, inc=1, device_id={"band": neighbour}, device_id_type=pl.DeviceIdType.MESH
        )
    pl.semaphore_wait(barrier, 2)
    copies = []
    for c in range(chunks):
        part = pl.ds(c * width, width)
        copies.append(
            pltpu.make_async_remote_copy(
                src_ref=pixels.at[0:SHIFT, part],
                dst_ref=nxt_buf.at[:, part],
                send_sem=send_sem.at[c],
                recv_sem=recv_sem.at[c],
                device_id={"band": left},
                device_id_type=pl.DeviceIdType.MESH,
            )
        )
    copies.append(
        pltpu.make_async_remote_copy(
            src_ref=pixels.at[rows - SHIFT : rows],
            dst_ref=prv_buf,
            send_sem=send_sem.at[chunks],
            recv_sem=recv_sem.at[chunks],
            device_id={"band": right},
            device_id_type=pl.DeviceIdType.MESH,
        )
    )
    copies.append(
        pltpu.make_async_remote_copy(
            src_ref=told,
            dst_ref=facts_buf,
            send_sem=send_sem.at[chunks + 1],
            recv_sem=recv_sem.at[chunks + 1],
            device_id={"band": right},
            device_id_type=pl.DeviceIdType.MESH,
        )
    )
    for copy in copies[:chunks]:
        copy.start()
    copies[chunks + 1].start()

    shifted[0 : WIN - SHIFT] = roll_cols(pixels[SHIFT:].astype(F32), SHIFT)
    bias_own[0], bias_own[1] = biases(bias, me == bands - 1, TOK)

    def step(i, _):
        def edge(g):
            return bias_own[(i * GROUP + g == windows - 1).astype(jnp.int32)]

        own = attend(group_at(shifted, i), gain_a[...], wq[...], wk[...], wv[...], wp[...], edge, TOK)
        for g in range(GROUP):
            w = i * GROUP + g
            value = own[g * TOK : (g + 1) * TOK]
            upper[w] = value[:HALF]
            first[w] = value[:, :LANES]
            rest[w] = value[:, LANES:]
        return 0

    for c in range(chunks):
        copies[c].wait()
        if c == chunks // 2:
            copies[chunks].start()
        low = c * width
        block = nxt_buf[:, low : low + width].astype(F32)
        if c == 0:
            shifted[WIN - SHIFT :, cols - SHIFT :] = block[:, :SHIFT]
            shifted[WIN - SHIFT :, 0 : width - SHIFT] = block[:, SHIFT:]
        else:
            shifted[WIN - SHIFT :, low - SHIFT : low + width - SHIFT] = block
        begin = 2 * c - 1 if c else 0
        end = 2 * c + 1 if c < chunks - 1 else groups
        lax.fori_loop(begin, end, step, 0)
    copies[chunks + 1].wait()
    facts[...] = facts_buf[...]
    copies[chunks].wait()
    prv[...] = prv_buf[...]


def pack_kernel(keep, count, dests, slots, first, rest, outgoing, order):
    bands = lax.axis_size("band")
    windows = first.shape[0]
    tiles = windows // TILE
    pairs = -(-tiles // bands)

    def scan(w, kept):
        order[kept] = w
        return kept + keep[w]

    live = jnp.minimum(lax.fori_loop(0, windows, scan, jnp.int32(0)), count[0])
    if bands * pairs > tiles:
        outgoing[...] = jnp.full(outgoing.shape, CAP, BF)
    lane = lax.broadcasted_iota(jnp.int32, (TOK, LANES), 1)

    def pack(t, _):
        place = dests[t] * pairs + t // bands
        slot = jnp.where(t * TILE < live, slots[t], CAP).astype(F32)
        halves = []
        for p in range(TILE):
            position = t * TILE + p
            valid = position < live
            source = jnp.where(valid, order[jnp.where(valid, position, 0)], 0)
            value = first[source]
            outgoing[place, p * TOK : (p + 1) * TOK] = jnp.where(valid, value, jnp.zeros_like(value))
            tail = rest[source].astype(F32)
            tail = jnp.concatenate([tail, jnp.zeros((TOK, 2 * LANES - CHAN), F32)], axis=1)
            halves.append(jnp.where(valid, tail, 0.0))
        both = jnp.where(lane < TOK, halves[0], pltpu.roll(halves[1], TOK, 1))
        both = jnp.where(lane >= SLOT_LANE, slot, both)
        outgoing[place, TILE * TOK :] = both.astype(BF)
        return 0

    lax.fori_loop(0, tiles, pack, 0)


def map_kernel(
    keep_own, count, facts, pixels, prv, upper, bias, gain_a, wq, wk, wv, wp, gain_m, wh, wo,
    restored,
    shifted, result, bias_prev, act_own, act_prev,
):
    me = lax.axis_index("band")
    windows = pixels.shape[1] // WIN

    def scan(w, carry):
        own, prev = carry
        act_own[w] = ((keep_own[w] == 1) & (own < count[0])).astype(jnp.int32)
        act_prev[w] = ((facts[0, w] == 1) & (prev < facts[0, windows])).astype(jnp.int32)
        return own + keep_own[w], prev + facts[0, w]

    lax.fori_loop(0, windows, scan, (jnp.int32(0), jnp.int32(0)))
    shifted[0:SHIFT] = roll_cols(prv[...].astype(F32), SHIFT)
    shifted[SHIFT:] = roll_cols(pixels[...].astype(F32), SHIFT)
    bias_prev[0], bias_prev[1] = biases(bias, me == 0, HALF)

    def step(i, _):
        def edge(g):
            return bias_prev[(i * GROUP + g == windows - 1).astype(jnp.int32)]

        prev = attend(group_at(shifted, i), gain_a[...], wq[...], wk[...], wv[...], wp[...], edge, HALF)
        states = jnp.concatenate([upper[i * GROUP + g] for g in range(GROUP)] + [prev], axis=0)
        done = feed(states, gain_m[...], wh[...], wo[...]).astype(F32)
        for g in range(GROUP):
            w = i * GROUP + g
            cols = pl.ds(pl.multiple_of(w * WIN, WIN), WIN)
            upper_new = done[g * HALF : (g + 1) * HALF].reshape(SHIFT, WIN, CHAN)
            lower_new = done[(GROUP + g) * HALF : (GROUP + g + 1) * HALF].reshape(SHIFT, WIN, CHAN)
            result[0:SHIFT, cols, :] = jnp.where(
                act_prev[w] == 1, lower_new, shifted[SHIFT : 2 * SHIFT, cols, :]
            )
            result[SHIFT:, cols, :] = jnp.where(
                act_own[w] == 1, upper_new, shifted[2 * SHIFT :, cols, :]
            )
        return 0

    lax.fori_loop(0, windows // GROUP, step, 0)
    restored[...] = roll_cols(result[...], -SHIFT).astype(BF)


def place_kernel(incoming, work):
    work[...] = jnp.zeros(work.shape, BF)
    lane = lax.broadcasted_iota(jnp.int32, (16, LANES), 1)

    def put(t, _):
        head = incoming[t, TILE * TOK : TILE * TOK + 16].astype(F32)
        slot = jnp.max(jnp.where(lane >= SLOT_LANE, head, 0.0)).astype(jnp.int32)

        @pl.when(slot < CAP)
        def _():
            tail = incoming[t, TILE * TOK :].astype(F32)
            work[slot, :, :LANES] = incoming[t, : TILE * TOK]
            work[slot, :TOK, LANES:] = tail[:, : CHAN - LANES].astype(BF)
            work[slot, TOK:, LANES:] = pltpu.roll(tail, TOK, 1)[:, : CHAN - LANES].astype(BF)

        return 0

    lax.fori_loop(0, incoming.shape[0], put, 0)


def position_bias(bias_table):
    coords = jnp.arange(TOK, dtype=jnp.int32)
    row_pos, col_pos = coords // WIN, coords % WIN
    index = (row_pos[:, None] - row_pos[None, :] + WIN - 1) * (2 * WIN - 1) + (
        col_pos[:, None] - col_pos[None, :] + WIN - 1
    )
    entries = bias_table.shape[0]
    onehot = (jnp.arange(entries, dtype=jnp.int32)[:, None] == index.reshape(1, -1)).astype(F32)
    return jnp.dot(bias_table.T, onehot, precision=lax.Precision.HIGHEST).reshape(HEADS, TOK, TOK)


def shards(
    pixels, keep_mask, band_counts, plan_dest, plan_slot, bias_table, gain_attn, qkv_weight,
    proj_weight, gain_mlp, hidden_weight, output_weight,
):
    bands = lax.axis_size("band")
    rows, cols, channels = pixels.shape
    windows = cols // WIN
    tiles = windows // TILE
    pairs = -(-tiles // bands)
    told = jnp.concatenate([keep_mask[0], band_counts])
    told = jnp.pad(told, (0, -told.shape[0] % LANES))[None]
    bias = position_bias(bias_table)
    wq, wk, wv = (qkv_weight[:, i * CHAN : (i + 1) * CHAN] for i in range(3))
    smem = pl.BlockSpec(memory_space=pltpu.SMEM)
    vmem = pl.BlockSpec(memory_space=pltpu.VMEM)
    limit = pltpu.CompilerParams(vmem_limit_bytes=63 * 1024 * 1024)
    chunks = windows // GROUP // 2
    upper, first, rest, prv, facts = pl.pallas_call(
        own_kernel,
        out_shape=(
            jax.ShapeDtypeStruct((windows, HALF, channels), BF),
            jax.ShapeDtypeStruct((windows, TOK, LANES), BF),
            jax.ShapeDtypeStruct((windows, TOK, channels - LANES), BF),
            jax.ShapeDtypeStruct((SHIFT, cols, channels), BF),
            jax.ShapeDtypeStruct(told.shape, jnp.int32),
        ),
        in_specs=[vmem] * 8,
        out_specs=(vmem,) * 5,
        scratch_shapes=[
            pltpu.VMEM((rows, cols, channels), F32),
            pltpu.VMEM((SHIFT, cols, channels), BF),
            pltpu.VMEM((SHIFT, cols, channels), BF),
            pltpu.VMEM(told.shape, jnp.int32),
            pltpu.VMEM((2, HEADS * TOK, TOK), F32),
            pltpu.SemaphoreType.DMA((chunks + 2,)),
            pltpu.SemaphoreType.DMA((chunks + 2,)),
        ],
        compiler_params=pltpu.CompilerParams(
            vmem_limit_bytes=63 * 1024 * 1024, collective_id=0, has_side_effects=True
        ),
        cost_estimate=pl.CostEstimate(flops=3 * 10**9, bytes_accessed=10**7, transcendentals=10**6),
        name="own",
    )(pixels, told, bias, gain_attn[None], wq, wk, wv, proj_weight)
    outgoing = pl.pallas_call(
        pack_kernel,
        out_shape=jax.ShapeDtypeStruct((bands * pairs, TILE * TOK + TOK, LANES), BF),
        in_specs=[smem] * 4 + [vmem] * 2,
        out_specs=vmem,
        scratch_shapes=[pltpu.SMEM((windows + 1,), jnp.int32)],
        compiler_params=limit,
        name="pack",
    )(keep_mask[0], band_counts, plan_dest[0], plan_slot[0], first, rest)
    incoming = lax.all_to_all(
        outgoing.reshape(bands, -1, LANES), "band", split_axis=0, concat_axis=0, tiled=True
    ).reshape(outgoing.shape)
    restored = pl.pallas_call(
        map_kernel,
        out_shape=jax.ShapeDtypeStruct((rows, cols, channels), BF),
        in_specs=[smem] * 3 + [vmem] * 12,
        out_specs=vmem,
        scratch_shapes=[
            pltpu.VMEM((rows + SHIFT, cols, channels), F32),
            pltpu.VMEM((rows, cols, channels), F32),
            pltpu.VMEM((2, HEADS * HALF, TOK), F32),
            pltpu.SMEM((windows,), jnp.int32),
            pltpu.SMEM((windows,), jnp.int32),
        ],
        compiler_params=limit,
        cost_estimate=pl.CostEstimate(flops=10**10, bytes_accessed=3 * 10**7, transcendentals=10**6),
        name="map",
    )(
        keep_mask[0], band_counts, facts, pixels, prv, upper, bias, gain_attn[None], wq, wk, wv,
        proj_weight, gain_mlp[None], hidden_weight, output_weight.T,
    )
    work = pl.pallas_call(
        place_kernel,
        out_shape=jax.ShapeDtypeStruct((CAP, TILE * TOK, channels), BF),
        in_specs=[vmem],
        out_specs=vmem,
        compiler_params=pltpu.CompilerParams(vmem_limit_bytes=16 * 1024 * 1024),
        name="place",
    )(incoming)
    return restored, work


def solution(mesh):
    split = P(("img", "band"))
    in_specs = (split,) * 5 + (P(),) * 7
    return jax.shard_map(shards, mesh=mesh, in_specs=in_specs, out_specs=(split, split), check_vma=False)
```

profile of v0, /device:TPU:0, one launch (start us, length us, event | category | flops | bytes accessed | tf_op | source)
XLA Modules:
  0.0 73.1 jit_solution(2091677623498159824)
XLA Ops:
  0.6 0.0 copy-start
  0.6 0.0 copy-start.2
  0.7 0.0 copy-start.1
  1.4 0.7 %pad_add_fusion = s32[33]{0:T(128)S(1)} fusion(s32[1]{0:T(128)S(6)} %copy.18.count, s32[32]{0:T(128)} %bitcast.17), kind=kLoop, calls=%fused_computation.9 | loop fusion | flops 33 | bytes 264 | tf_op jit(solution)/shard_map/concatenate | solution.py:325
  2.1 0.6 pad_bitcast_fusion.told
  2.7 0.1 add_add_fusion
  2.8 0.1 add.57
  2.9 0.0 copy-done
  2.9 1.3 %convolution_bitcast_fusion = f32[6,4096]{1,0:T(8,128)S(1)} fusion(f32[225,6]{0,1:T(8,128)S(1)} %copy-done, s32[4096]{0:T(1024)S(1)} %add.57), kind=kOutput, calls=%fused_computation | convolution fusion | flops 67276800 | bytes 120088 | tf_op jit(solution)/shard_map/dot_general | solution.py:313
  4.2 0.8 %reshape.97.bias = f32[6,64,64]{2,1,0:T(8,128)} reshape(f32[6,4096]{1,0:T(8,128)S(1)} %convolution_bitcast_fusion) | data formatting | bytes 196608 | tf_op jit(solution)/shard_map/reshape | solution.py:313
  5.0 0.0 copy-done.2
  5.0 0.8 %fusion.1 = (bf16[180,180]{1,0:T(8,128)(2,1)}, bf16[180,180]{1,0:T(8,128)(2,1)}, bf16[180,180]{1,0:T(8,128)(2,1)}) fusion(bf16[180,540]{1,0:T(8,128)(2,1)S(1)} %copy-done.2), kind=kLoop, calls=%fused_computation.11 | loop fusion | bytes 388800 | tf_op jit(solution)/shard_map/slice | solution.py:328
  5.8 0.0 copy-done.1
  5.8 1.5 %copy.14.pixels = bf16[8,256,180]{2,1,0:T(8,128)(2,1)} copy(bf16[8,256,180]{1,0,2:T(8,128)(2,1)S(1)} %copy-done.1) | data formatting | bytes 1474560 | tf_op args[0]
  7.2 33.8 %own.1 = (bf16[32,32,180]{2,1,0:T(8,128)(2,1)}, bf16[32,64,128]{2,1,0:T(8,128)(2,1)}, bf16[32,64,52]{2,1,0:T(8,128)(2,1)}, bf16[4,256,180]{2,1,0:T(8,128)(2,1)}, s32[1,128]{1,0:T(1,128)}) custom-call(bf16[8,256,180]{2,1,0:T(8,128)(2,1)} %copy.14.pixels, s32[1,128]{1,0:T(1,128)} %pad_bitcast_fusion.told, f32[6,64,64]{2,1,0:T(8,128)} %reshape.97.bias, ...), custom_call_target="tpu_custom_call" | custom-call | flops 3000000000 | bytes 10000000 | tf_op jit(solution)/shard_map/own/pallas_call | solution.py:333
  41.0 3.6 %pack.1 = bf16[16,192,128]{2,1,0:T(8,128)(2,1)} custom-call(s32[32]{0:T(128)} %bitcast.18, s32[1]{0:T(128)S(6)} %copy.18.count, s32[16]{0:T(128)} %bitcast.15, s32[16]{0:T(128)} %bitcast.16, bf16[32,64,128]{2,1,0:T(8,128)(2,1)} %get-tuple-element.10.first, bf16[32,64,52]{2,1,0:T(8,128)(2,1)} %get-tuple-element.11.rest), custom_call_target="tpu_custom_call" | custom-call | tf_op jit(solution)/shard_map/pack/pallas_call | solution.py:359
  44.6 5.0 %all-to-all-start = ((bf16[8,384,128]{2,1,0:T(8,128)(2,1)}), bf16[8,384,128]{2,1,0:T(8,128)(2,1)S(1)}, u32[]{:S(2)}, u32[]{:S(2)}) async-start(bf16[8,384,128]{2,1,0:T(8,128)(2,1)} %bitcast.14), calls=%async_computation | async-start | bytes 1572864 | tf_op jit(solution)/shard_map/all_to_all | solution.py:368
  49.7 17.5 %map.1 = bf16[8,256,180]{2,1,0:T(8,128)(2,1)} custom-call(s32[32]{0:T(128)} %bitcast.19, s32[1]{0:T(128)S(6)} %copy.18.count, s32[1,128]{1,0:T(1,128)} %get-tuple-element.7.facts, bf16[8,256,180]{2,1,0:T(8,128)(2,1)} %copy.14.pixels, bf16[4,256,180]{2,1,0:T(8,128)(2,1)} %get-tuple-element.8.prv, bf16[32,32,180]{2,1,0:T(8,128)(2,1)} %get-tuple-element.9.upper, ...), custom_call_target="tpu_custom_call" | custom-call | flops 10000000000 | bytes 30000000 | tf_op jit(solution)/shard_map/map/pallas_call | solution.py:371
  67.1 2.3 %copy.16 = bf16[8,256,180]{1,0,2:T(8,128)(2,1)} copy(bf16[8,256,180]{2,1,0:T(8,128)(2,1)} %map.1) | data formatting | bytes 1474560
  69.4 0.0 all-to-all-done
  69.5 2.6 %place.1 = bf16[8,128,180]{2,1,0:T(8,128)(2,1)S(1)} custom-call(bf16[16,192,128]{2,1,0:T(8,128)(2,1)S(1)} %bitcast.13), custom_call_target="tpu_custom_call" | custom-call | tf_op jit(solution)/shard_map/place/pallas_call | solution.py:390
  72.1 1.0 %copy.17 = bf16[8,128,180]{1,0,2:T(8,128)(2,1)} copy(bf16[8,128,180]{2,1,0:T(8,128)(2,1)S(1)} %place.1) | data formatting | bytes 737280
  (1 shorter events, 0.0 us)
Async XLA Ops:
  0.6 2.2 %copy-start = (f32[225,6]{0,1:T(8,128)S(1)}, f32[225,6]{0,1:T(8,128)}, u32[]{:S(2)}) copy-start(f32[225,6]{0,1:T(8,128)} %param.17) | copy-start | bytes 16204
  0.6 4.3 %copy-start.2 = (bf16[180,540]{1,0:T(8,128)(2,1)S(1)}, bf16[180,540]{1,0:T(8,128)(2,1)}, u32[]{:S(2)}) copy-start(bf16[180,540]{1,0:T(8,128)(2,1)} %param.19) | copy-start | bytes 583204
  0.7 5.1 %copy-start.1 = (bf16[8,256,180]{1,0,2:T(8,128)(2,1)S(1)}, bf16[8,256,180]{1,0,2:T(8,128)(2,1)}, u32[]{:S(2)}) copy-start(bf16[8,256,180]{1,0,2:T(8,128)(2,1)} %param.12) | copy-start | bytes 2211844
  44.6 24.8 %all-to-all-start = ((bf16[8,384,128]{2,1,0:T(8,128)(2,1)}), bf16[8,384,128]{2,1,0:T(8,128)(2,1)S(1)}, u32[]{:S(2)}, u32[]{:S(2)}) async-start(bf16[8,384,128]{2,1,0:T(8,128)(2,1)} %bitcast.14), calls=%async_computation | async-start | bytes 1572864 | tf_op jit(solution)/shard_map/all_to_all | solution.py:368
where the time goes:
time: 73.4 us; the launch traced here: 73.1 us
  Pallas kernels  57.5 us (78%)
  local copies, waits for them, and re-layouts  7.03 us (10%)
  starting transfers between devices  5.03 us (7%)
  between operations  1.42 us (2%)
  matrix products  1.3 us (2%)
  other arithmetic  0.81 us (1%)
    pallas_call x1, Pallas kernels, shards(): pl.pallas_call(own_kernel, out_shape=(jax.ShapeDtypeStruct((windows, HALF...  33.8 us
    pallas_call x1, Pallas kernels, shards(): pl.pallas_call(map_kernel, out_shape=jax.ShapeDtypeStruct((rows, cols, ch...  17.5 us
    all_to_all x1, starting transfers between devices, shards(): lax.all_to_all(outgoing.reshape(bands, -1, LANES), 'band', split_axis=0,...  5.03 us
    unnamed x9, local copies, waits for them, and re-layouts  4.81 us
    pallas_call x1, Pallas kernels, shards(): pl.pallas_call(pack_kernel, out_shape=jax.ShapeDtypeStruct((bands * pairs...  3.61 us
    pallas_call x1, Pallas kernels, shards(): pl.pallas_call(place_kernel, out_shape=jax.ShapeDtypeStruct((CAP, TILE *...  2.62 us
  transfers between devices with their start and end apart: 1, of which 0 were waited for; matrix products, arithmetic and copies ran while one was open for 3% of the time, Pallas kernels for 24%

commit v1 on v0

v1 whole, which is shorter than its diff:
```python
import jax
import jax.numpy as jnp
from jax import lax
from jax.experimental import pallas as pl
from jax.experimental.pallas import tpu as pltpu
from jax.sharding import PartitionSpec as P

CHAN = 180
HEADS = 6
WIN = 8
TILE = 2
SHIFT = 4
CAP = 8
TOK = WIN * WIN
HALF = TOK // 2
HEAD_DIM = CHAN // HEADS
GROUP = 4
LANES = 128
SLOT_LANE = 120

EPSILON = 1e-05
BF = jnp.bfloat16
F32 = jnp.float32


def layer_norm(values, gain_vec):
    center = values - jnp.sum(values, axis=-1, keepdims=True) * (1.0 / CHAN)
    spread = jnp.sum(center * center, axis=-1, keepdims=True) * (1.0 / CHAN)
    return (center * lax.rsqrt(spread + EPSILON) * gain_vec).astype(BF)


def dot(a, b):
    return jnp.dot(a, b, preferred_element_type=F32)


def dot_t(a, b):
    return lax.dot_general(a, b, (((1,), (1,)), ((), ())), preferred_element_type=F32)


def bias_strips(table, strips):
    heads, entries = table.shape
    values = jnp.concatenate([table[...], jnp.zeros((8 - heads, entries), F32)], axis=0)
    high = values.astype(BF).astype(F32)
    middle = (values - high).astype(BF).astype(F32)
    low = values - high - middle
    parts = jnp.concatenate([high, middle, low], axis=0).astype(BF)
    shape = (entries, WIN * LANES)
    entry = lax.broadcasted_iota(jnp.int32, shape, 0)
    lane = lax.broadcasted_iota(jnp.int32, shape, 1)
    step = (lane % LANES) // WIN
    wanted = (2 * WIN - 2 - step) * (2 * WIN - 1) + lane // LANES - lane % WIN + WIN - 1
    pick = jnp.where((entry == wanted) & (step < 2 * WIN - 1), 1.0, 0.0).astype(BF)
    found = dot(parts, pick)
    found = found[0:8] + found[8:16] + found[16:24]
    for c in range(WIN):
        strips[pl.ds(c, 8, stride=WIN), :] = found[:, c * LANES : (c + 1) * LANES]


def bias_base(strips, queries):
    tiles = []
    for h in range(HEADS):
        strip = strips[h * WIN : (h + 1) * WIN, :]
        for r in range(WIN - queries // WIN, WIN):
            by = (WIN - 1 - r) * WIN
            tiles.append(pltpu.roll(strip, (LANES - by) % LANES, 1)[:, :TOK])
    return jnp.concatenate(tiles, axis=0)


def biases(strips, last_row, queries):
    first = TOK - queries
    base = bias_base(strips, queries)
    shape = (HEADS * queries, TOK)
    key = lax.broadcasted_iota(jnp.int32, shape, 1)
    query = lax.broadcasted_iota(jnp.int32, shape, 0) % queries + first
    rows_differ = (key // WIN >= SHIFT) != (query // WIN >= SHIFT)
    cols_differ = (key % WIN >= SHIFT) != (query % WIN >= SHIFT)
    row_pen = jnp.where(rows_differ, jnp.where(last_row, -100.0, 0.0).astype(F32), 0.0)
    plain = base + row_pen
    both = base + jnp.where(cols_differ, -100.0, row_pen)
    return plain, both


def head_masks():
    lane = lax.broadcasted_iota(jnp.int32, (1, CHAN), 1)
    return [
        ((lane >= h * HEAD_DIM) & (lane < (h + 1) * HEAD_DIM)).astype(F32) for h in range(HEADS)
    ]


def attend(x, gain, wq, wk, wv, wp, bias_of, queries):
    masks = head_masks()
    low_masks = [m.astype(BF) for m in masks]
    normed = layer_norm(x, gain)
    if queries == TOK:
        x_q, n_q = x, normed
    else:
        pick = lambda a: jnp.concatenate(
            [a[g * TOK + TOK - queries : (g + 1) * TOK] for g in range(GROUP)], axis=0
        )
        x_q, n_q = pick(x), pick(normed)
    q = (dot(n_q, wq) * HEAD_DIM ** (-0.5)).astype(BF)
    k = dot(normed, wk).astype(BF)
    v = dot(normed, wv).astype(BF)
    mixed = []
    for g in range(GROUP):
        q_w = q[g * queries : (g + 1) * queries]
        stacked = jnp.concatenate([q_w * low_masks[h] for h in range(HEADS)], axis=0)
        scores = dot_t(stacked, k[g * TOK : (g + 1) * TOK]) + bias_of(g)
        top = jnp.max(scores, axis=1, keepdims=True)
        grown = jnp.exp(scores - top)
        weights = (grown * (1.0 / jnp.sum(grown, axis=1, keepdims=True))).astype(BF)
        wide = dot(weights, v[g * TOK : (g + 1) * TOK])
        total = wide[:queries] * masks[0]
        for h in range(1, HEADS):
            total = total + wide[h * queries : (h + 1) * queries] * masks[h]
        mixed.append(total)
    mixed = jnp.concatenate(mixed, axis=0).astype(BF)
    return (x_q + dot(mixed, wp)).astype(BF)


def feed(states, gain, wh, wo):
    flat = states.astype(F32)
    normed = layer_norm(flat, gain)
    inner = jax.nn.gelu(dot(normed, wh)).astype(BF)
    return (flat + dot_t(inner, wo)).astype(BF)


def window_at(image, i, g, row):
    start = pl.multiple_of((i * GROUP + g) * WIN, WIN)
    return image[row : row + WIN, pl.ds(start, WIN), :].reshape(TOK, CHAN)


def group_at(image, i, row):
    return jnp.concatenate([window_at(image, i, g, row) for g in range(GROUP)], axis=0)


def plane_row(planes, row, channels):
    halves = planes.shape[0]
    return jnp.concatenate(
        [planes[h, pl.ds(row, channels, stride=WIN), :] for h in range(halves)], axis=1
    )


def block_kernel(
    keep, count, dests, slots, keep_row, pixels, table, gain_a, wqkv, wp, gain_m, wh, wo,
    restored, incoming,
    planes, image, nxt_out, prv_out, nxt_buf, prv_buf, told, told_buf, weights, strips,
    bias_own, bias_prev, first, rest, upper, result, active, outgoing, following, order,
    halo_send, halo_recv, tile_send, tile_recv,
):
    bands = lax.axis_size("band")
    me = lax.axis_index("band")
    right, left = lax.rem(me + 1, bands), lax.rem(me + bands - 1, bands)
    channels, rows, cols = pixels.shape
    windows = cols // WIN
    groups = windows // GROUP
    halves = cols // LANES
    tiles = windows // TILE
    pairs = -(-tiles // bands)
    span = min(bands, tiles)
    mesh_id = pl.DeviceIdType.MESH

    barrier = pltpu.get_barrier_semaphore()

    def greet(i, _):
        peer = lax.rem(me + i, bands)
        pl.semaphore_signal(barrier, inc=1, device_id={"band": peer}, device_id_type=mesh_id)
        return 0

    lax.fori_loop(1, bands, greet, 0)

    for h in range(halves):
        part = pixels[:, :, h * LANES : (h + 1) * LANES].astype(F32)
        planes[h] = part.reshape(channels * rows, LANES)
    for r in range(SHIFT):
        nxt_out[r] = pltpu.roll(plane_row(planes, r, channels), cols - SHIFT, 1).astype(BF)
    pl.semaphore_wait(barrier, bands - 1)

    def nxt_copy(c):
        part = pl.ds(pl.multiple_of(c * LANES, LANES), LANES)
        return pltpu.make_async_remote_copy(
            src_ref=nxt_out.at[:, :, part],
            dst_ref=nxt_buf.at[:, :, part],
            send_sem=halo_send.at[c],
            recv_sem=halo_recv.at[c],
            device_id={"band": left},
            device_id_type=mesh_id,
        )

    prv_copy = pltpu.make_async_remote_copy(
        src_ref=prv_out,
        dst_ref=prv_buf,
        send_sem=halo_send.at[halves],
        recv_sem=halo_recv.at[halves],
        device_id={"band": right},
        device_id_type=mesh_id,
    )
    told_copy = pltpu.make_async_remote_copy(
        src_ref=told,
        dst_ref=told_buf,
        send_sem=halo_send.at[halves + 1],
        recv_sem=halo_recv.at[halves + 1],
        device_id={"band": right},
        device_id_type=mesh_id,
    )
    for c in range(halves):
        nxt_copy(c).start()

    for r in range(rows):
        row = pltpu.roll(plane_row(planes, r, channels), cols - SHIFT, 1)
        if r >= rows - SHIFT:
            prv_out[r - rows + SHIFT] = row.astype(BF)
        image[SHIFT + r] = row.T
    for i in range(3):
        weights[i] = wqkv[:, i * CHAN : (i + 1) * CHAN]
    bias_strips(table, strips)
    bias_own[0], bias_own[1] = biases(strips, me == bands - 1, TOK)
    bias_prev[0], bias_prev[1] = biases(strips, me == 0, HALF)

    told[...] = jnp.zeros(told.shape, jnp.int32)
    told[:, 0:windows] = jnp.broadcast_to(keep_row[...], (8, windows))
    kept = told[...]
    tri = (LANES, LANES)
    before = lax.broadcasted_iota(jnp.int32, tri, 0) < lax.broadcasted_iota(jnp.int32, tri, 1)
    place = dot(kept.astype(F32).astype(BF), jnp.where(before, 1.0, 0.0).astype(BF))
    told[...] = jnp.where(place < count[0].astype(F32), kept, 0)

    def spread(flags):
        own_lane = (windows, LANES)
        diagonal = lax.broadcasted_iota(jnp.int32, own_lane, 0) == lax.broadcasted_iota(
            jnp.int32, own_lane, 1
        )
        chosen = jnp.where(diagonal, jnp.broadcast_to(flags[0:1].astype(F32), own_lane), 0.0)
        return dot(chosen.astype(BF), jnp.ones((LANES, channels), BF))

    active[0] = spread(told[...])

    following[windows] = jnp.int32(windows)

    def scan(i, kept_so_far):
        w = windows - 1 - i
        following[w] = jnp.where(keep[0, w] == 1, w, following[w + 1])
        return kept_so_far + keep[0, w]

    live = jnp.minimum(lax.fori_loop(0, windows, scan, jnp.int32(0)), count[0])

    def rank(p, window):
        order[p] = jnp.minimum(window, windows - 1)
        return following[jnp.minimum(window + 1, windows)]

    lax.fori_loop(0, windows, rank, following[0])

    def step(i, _):
        def edge(g):
            return bias_own[(i * GROUP + g == windows - 1).astype(jnp.int32)]

        own = attend(
            group_at(image, i, WIN), gain_a[...], weights[0], weights[1], weights[2], wp[...],
            edge, TOK,
        )
        wide = own.astype(F32)
        for g in range(GROUP):
            w = i * GROUP + g
            upper[w] = own[g * TOK : g * TOK + HALF]
            first[w] = own[g * TOK : (g + 1) * TOK, :LANES]
            tail = wide[g * TOK : (g + 1) * TOK, LANES:]
            rest[w] = jnp.concatenate([tail, jnp.zeros((TOK, 2 * LANES - CHAN), F32)], axis=1)
        return 0

    for c in range(halves):
        nxt_copy(c).wait()
        if c == halves - 1:
            told_copy.start()
            prv_copy.start()
        for r in range(SHIFT):
            block = nxt_buf[r, :, c * LANES : (c + 1) * LANES].astype(F32)
            image[SHIFT + rows + r, c * LANES : (c + 1) * LANES, :] = block.T
        lax.fori_loop(c * groups // halves, (c + 1) * groups // halves, step, 0)

    lane = lax.broadcasted_iota(jnp.int32, (TOK, LANES), 1)

    def pack(index, peer, j):
        t = jnp.int32(0)
        found = jnp.int32(0)
        for i in range(span):
            hit = dests[0, j * span + i] == peer
            t = jnp.where(hit, j * span + i, t)
            found = jnp.where(hit, 1, found)
        live_tile = (found > 0) & (t * TILE < live)
        slot = jnp.where(live_tile, slots[0, t], CAP).astype(F32)
        halves_of = []
        for p in range(TILE):
            position = t * TILE + p
            valid = live_tile & (position < live)
            source = order[position]
            value = first[source]
            outgoing[index, p * TOK : (p + 1) * TOK] = jnp.where(valid, value, jnp.zeros_like(value))
            halves_of.append(jnp.where(valid, rest[source], 0.0))
        both = jnp.where(lane < TOK, halves_of[0], pltpu.roll(halves_of[1], TOK, 1))
        outgoing[index, TILE * TOK :] = jnp.where(lane >= SLOT_LANE, slot, both).astype(BF)

    def tile_copy(i):
        return pltpu.make_async_remote_copy(
            src_ref=outgoing.at[pl.ds(i * pairs, pairs)],
            dst_ref=incoming.at[pl.ds(me * pairs, pairs)],
            send_sem=tile_send.at[i],
            recv_sem=tile_recv.at[i],
            device_id={"band": lax.rem(me + i, bands)},
            device_id_type=mesh_id,
        )

    def dispatch(i, _):
        for j in range(pairs):
            pack(i * pairs + j, lax.rem(me + i, bands), j)
        tile_copy(i).start()
        return 0

    lax.fori_loop(1, bands, dispatch, 0)
    for j in range(pairs):
        pack(j, me, j)
    incoming[pl.ds(me * pairs, pairs)] = outgoing[0:pairs]

    def blend(done, flags, w, row):
        cols_w = pl.ds(pl.multiple_of(w * WIN, WIN), WIN)
        chosen = active[flags, pl.ds(w, 1), :].reshape(1, 1, channels) > 0.5
        value = done.reshape(SHIFT, WIN, CHAN)
        result[row : row + SHIFT, cols_w, :] = jnp.where(
            chosen, value, image[SHIFT + row : 2 * SHIFT + row, cols_w, :]
        )

    def finish_own(i, _):
        span_w = 2 * GROUP
        states = jnp.concatenate([upper[i * span_w + g] for g in range(span_w)], axis=0)
        done = feed(states, gain_m[...], wh[...], wo[...]).astype(F32)
        for g in range(span_w):
            blend(done[g * HALF : (g + 1) * HALF], 0, i * span_w + g, SHIFT)
        return 0

    lax.fori_loop(0, groups // 2, finish_own, 0)

    told_copy.wait()
    active[1] = spread(told_buf[...])
    prv_copy.wait()
    for r in range(SHIFT):
        image[r] = prv_buf[r].astype(F32).T

    def finish_prev(i, _):
        def edge(g):
            return bias_prev[(i * GROUP + g == windows - 1).astype(jnp.int32)]

        prev = attend(
            group_at(image, i, 0), gain_a[...], weights[0], weights[1], weights[2], wp[...],
            edge, HALF,
        )
        done = feed(prev, gain_m[...], wh[...], wo[...]).astype(F32)
        for g in range(GROUP):
            blend(done[g * HALF : (g + 1) * HALF], 1, i * GROUP + g, 0)
        return 0

    lax.fori_loop(0, groups, finish_prev, 0)
    for r in range(rows):
        row = pltpu.roll(result[r].T, SHIFT, 1)
        for h in range(halves):
            planes[h, pl.ds(r, channels, stride=WIN), :] = row[:, h * LANES : (h + 1) * LANES]
    for h in range(halves):
        restored[:, :, h * LANES : (h + 1) * LANES] = (
            planes[h].reshape(channels, rows, LANES).astype(BF)
        )

    def collect(i, _):
        tile_copy(i).wait()
        return 0

    lax.fori_loop(1, bands, collect, 0)


def place_kernel(incoming, work, planes):
    total = incoming.shape[0]
    channels = work.shape[0]
    head = jnp.max(incoming[:, TILE * TOK : TILE * TOK + 16, :].astype(F32), axis=1)
    lane = lax.broadcasted_iota(jnp.int32, (total, LANES), 1)
    slot = jnp.max(jnp.where(lane >= SLOT_LANE, head, 0.0), axis=1, keepdims=True).astype(jnp.int32)
    match = slot == lane
    index = lax.broadcasted_iota(jnp.int32, (total, LANES), 0)
    source = jnp.max(jnp.where(match, index, -1).astype(F32), axis=0, keepdims=True).astype(jnp.int32)
    for k in range(CAP):
        known = source[0, k] >= 0
        t = jnp.maximum(source[0, k], 0)
        main = incoming[t, : TILE * TOK].astype(F32)
        tail = incoming[t, TILE * TOK :].astype(F32)
        tails = jnp.concatenate([tail, pltpu.roll(tail, TOK, 1)], axis=0)
        block = jnp.concatenate([main.T, tails.T[: channels - LANES]], axis=0)
        planes[pl.ds(k, channels, stride=CAP), :] = jnp.where(known, block, 0.0)
    work[...] = planes[...].reshape(channels, CAP, TILE * TOK).astype(BF)


def shards(
    pixels, keep_mask, band_counts, plan_dest, plan_slot, bias_table, gain_attn, qkv_weight,
    proj_weight, gain_mlp, hidden_weight, output_weight,
):
    bands = lax.axis_size("band")
    rows, cols, channels = pixels.shape
    windows = cols // WIN
    halves = cols // LANES
    tiles = windows // TILE
    pairs = -(-tiles // bands)
    smem = pl.BlockSpec(memory_space=pltpu.SMEM)
    vmem = pl.BlockSpec(memory_space=pltpu.VMEM)
    tile_shape = (bands * pairs, TILE * TOK + TOK, LANES)
    restored, incoming = pl.pallas_call(
        block_kernel,
        out_shape=(
            jax.ShapeDtypeStruct((channels, rows, cols), BF),
            jax.ShapeDtypeStruct(tile_shape, BF),
        ),
        in_specs=[smem] * 4 + [vmem] * 9,
        out_specs=(vmem, vmem),
        scratch_shapes=[
            pltpu.VMEM((halves, channels * rows, LANES), F32),
            pltpu.VMEM((rows + 2 * SHIFT, cols, channels), F32),
            pltpu.VMEM((SHIFT, channels, cols), BF),
            pltpu.VMEM((SHIFT, channels, cols), BF),
            pltpu.VMEM((SHIFT, channels, cols), BF),
            pltpu.VMEM((SHIFT, channels, cols), BF),
            pltpu.VMEM((8, LANES), jnp.int32),
            pltpu.VMEM((8, LANES), jnp.int32),
            pltpu.VMEM((3, channels, channels), BF),
            pltpu.VMEM((8 * WIN, LANES), F32),
            pltpu.VMEM((2, HEADS * TOK, TOK), F32),
            pltpu.VMEM((2, HEADS * HALF, TOK), F32),
            pltpu.VMEM((windows, TOK, LANES), BF),
            pltpu.VMEM((windows, TOK, LANES), F32),
            pltpu.VMEM((windows, HALF, channels), BF),
            pltpu.VMEM((rows, cols, channels), F32),
            pltpu.VMEM((2, windows, channels), F32),
            pltpu.VMEM(tile_shape, BF),
            pltpu.SMEM((windows + 1,), jnp.int32),
            pltpu.SMEM((windows,), jnp.int32),
            pltpu.SemaphoreType.DMA((halves + 2,)),
            pltpu.SemaphoreType.DMA((halves + 2,)),
            pltpu.SemaphoreType.DMA((bands,)),
            pltpu.SemaphoreType.DMA((bands,)),
        ],
        compiler_params=pltpu.CompilerParams(
            vmem_limit_bytes=63 * 1024 * 1024, collective_id=0, has_side_effects=True
        ),
        cost_estimate=pl.CostEstimate(flops=10**10, bytes_accessed=10**7, transcendentals=10**6),
        name="block",
    )(
        keep_mask, band_counts, plan_dest, plan_slot, keep_mask, jnp.transpose(pixels, (2, 0, 1)),
        bias_table.T, gain_attn[None], qkv_weight, proj_weight, gain_mlp[None], hidden_weight,
        output_weight.T,
    )
    work = pl.pallas_call(
        place_kernel,
        out_shape=jax.ShapeDtypeStruct((channels, CAP, TILE * TOK), BF),
        in_specs=[vmem],
        out_specs=vmem,
        scratch_shapes=[pltpu.VMEM((channels * CAP, TILE * TOK), F32)],
        compiler_params=pltpu.CompilerParams(vmem_limit_bytes=16 * 1024 * 1024),
        name="place",
    )(incoming)
    return jnp.transpose(restored, (1, 2, 0)), jnp.transpose(work, (1, 2, 0))


def solution(mesh):
    split = P(("img", "band"))
    in_specs = (split,) * 5 + (P(),) * 7
    return jax.shard_map(shards, mesh=mesh, in_specs=in_specs, out_specs=(split, split), check_vma=False)
```

time: 73.4 us -> 53.8 us (0.73)
  Pallas kernels: 57.5 us -> 50.3 us
  local copies, waits for them, and re-layouts: 7.03 us -> 1.99 us
  starting transfers between devices: 5.03 us -> 0 us
  matrix products: 1.3 us -> 0 us
  other arithmetic: 0.81 us -> 0 us
    pallas_call x4 -> x2, Pallas kernels: 57.5 us -> 50.3 us  [the longest x1 49 us: shards(): pl.pallas_call(block_kernel, out_shape=(jax.ShapeDtypeStruct((channels, r...]
    all_to_all x1 -> x0, starting transfers between devices: 5.03 us -> none  [shards(): lax.all_to_all(outgoing.reshape(bands, -1, LANES), 'band', split_axis=0,...]
    unnamed x9 -> x5, local copies, waits for them, and re-layouts: 4.81 us -> 1.99 us
    dot_general x1 -> x0, matrix products: 1.3 us -> none  [position_bias(): jnp.dot(bias_table.T, onehot, precision=lax.Precision.HIGHEST)]
    slice x1 -> x0, local copies, waits for them, and re-layouts: 0.79 us -> none  [shards(): wq, wk, wv = (qkv_weight[:, i * CHAN:(i + 1) * CHAN] for i in range(3))]
    reshape x1 -> x0, local copies, waits for them, and re-layouts: 0.77 us -> none  [position_bias(): jnp.dot(bias_table.T, onehot, precision=lax.Precision.HIGHEST)]
  transfers between devices with their start and end apart: 1 -> 0, of which waited for: 0 -> 0; matrix products, arithmetic and copies ran while one was open for 3% -> 0% of each run, Pallas kernels for 24% -> 0%
where the time goes in v1:
time: 53.8 us; the launch traced here: 53.6 us
  Pallas kernels  50.3 us (93%)
  local copies, waits for them, and re-layouts  1.99 us (4%)
  between operations  1.3 us (2%)
    pallas_call x1, Pallas kernels, shards(): pl.pallas_call(block_kernel, out_shape=(jax.ShapeDtypeStruct((channels, r...  49 us
    unnamed x5, local copies, waits for them, and re-layouts  1.99 us
    pallas_call x1, Pallas kernels, shards(): pl.pallas_call(place_kernel, out_shape=jax.ShapeDtypeStruct((channels, CA...  1.34 us

profile of v1, /device:TPU:0, one launch (start us, length us, event | category | flops | bytes accessed | tf_op | source)
XLA Modules:
  0.0 53.6 jit_solution(13086673991936169756)
XLA Ops:
  1.3 49.0 %block.1 = (bf16[180,8,256]{2,1,0:T(8,128)(2,1)}, bf16[16,192,128]{2,1,0:T(8,128)(2,1)}) custom-call(s32[1,32]{1,0:T(1,128)} %keep_row.1, s32[1]{0:T(128)S(6)} %copy.15.count, s32[1,16]{1,0:T(1,128)} %dests.1, s32[1,16]{1,0:T(1,128)} %slots.1, s32[1,32]{1,0:T(1,128)} %keep_row.1, bf16[180,8,256]{2,1,0:T(8,128)(2,1)} %bitcast.9, f32[6,225]{1,0:T(8,128)} %bitcast.11, ...), custom_call_target="tpu_custom_call" | custom-call | flops 10000000000 | bytes 10000000 | tf_op jit(solution)/shard_map/block/pallas_call | solution.py:410
  50.3 0.0 copy-start
  50.3 1.1 %copy-done = bf16[16,192,128]{2,1,0:T(8,128)(2,1)S(1)} copy-done((bf16[16,192,128]{2,1,0:T(8,128)(2,1)S(1)}, bf16[16,192,128]{2,1,0:T(8,128)(2,1)}, u32[]{:S(2)}) %copy-start) | copy-done | bytes 786456
  51.4 0.0 copy-start.1
  51.4 1.3 %place.1 = bf16[180,8,128]{2,1,0:T(8,128)(2,1)} custom-call(bf16[16,192,128]{2,1,0:T(8,128)(2,1)S(1)} %copy-done), custom_call_target="tpu_custom_call" | custom-call | tf_op jit(solution)/shard_map/place/pallas_call | solution.py:454
  52.8 0.0 copy-done.1
  52.8 0.9 %copy.16 = bf16[8,256,180]{1,0,2:T(8,128)(2,1)} copy(bf16[8,256,180]{1,0,2:T(8,128)(2,1)S(1)} %bitcast.7) | data formatting | bytes 1474560
Async XLA Ops:
  50.3 1.1 %copy-start = (bf16[16,192,128]{2,1,0:T(8,128)(2,1)S(1)}, bf16[16,192,128]{2,1,0:T(8,128)(2,1)}, u32[]{:S(2)}) copy-start(bf16[16,192,128]{2,1,0:T(8,128)(2,1)} %get-tuple-element.5.incoming) | copy-start | bytes 2359300
  51.4 1.3 %copy-start.1 = (bf16[180,8,256]{2,1,0:T(8,128)(2,1)S(1)}, bf16[180,8,256]{2,1,0:T(8,128)(2,1)}, u32[]{:S(2)}) copy-start(bf16[180,8,256]{2,1,0:T(8,128)(2,1)} %get-tuple-element.4) | copy-start | bytes 2211844

commit v2 on v1

--- a/solution.py
+++ b/solution.py
@@ -14,7 +14,11 @@
 TOK = WIN * WIN
 HALF = TOK // 2
 HEAD_DIM = CHAN // HEADS
-GROUP = 4
+GROUP = 16
+SIZE = GROUP * TOK
+PAD = 32
+DEPTH = HEADS * PAD
+QUERIES = HEADS * TOK
 LANES = 128
 SLOT_LANE = 120
 
@@ -23,10 +27,10 @@
 F32 = jnp.float32
 
 
-def layer_norm(values, gain_vec):
-    center = values - jnp.sum(values, axis=-1, keepdims=True) * (1.0 / CHAN)
-    spread = jnp.sum(center * center, axis=-1, keepdims=True) * (1.0 / CHAN)
-    return (center * lax.rsqrt(spread + EPSILON) * gain_vec).astype(BF)
+def layer_norm(values, gain):
+    center = values - jnp.sum(values, axis=0, keepdims=True) * (1.0 / CHAN)
+    spread = jnp.sum(center * center, axis=0, keepdims=True) * (1.0 / CHAN)
+    return (center * lax.rsqrt(spread + EPSILON) * gain).astype(BF)
 
 
 def dot(a, b):
@@ -35,6 +39,10 @@
 
 def dot_t(a, b):
     return lax.dot_general(a, b, (((1,), (1,)), ((), ())), preferred_element_type=F32)
+
+
+def iota(shape, axis):
+    return lax.broadcasted_iota(jnp.int32, shape, axis)
 
 
 def bias_strips(table, strips):
@@ -45,10 +53,9 @@
     low = values - high - middle
     parts = jnp.concatenate([high, middle, low], axis=0).astype(BF)
     shape = (entries, WIN * LANES)
-    entry = lax.broadcasted_iota(jnp.int32, shape, 0)
-    lane = lax.broadcasted_iota(jnp.int32, shape, 1)
+    entry, lane = iota(shape, 0), iota(shape, 1)
     step = (lane % LANES) // WIN
-    wanted = (2 * WIN - 2 - step) * (2 * WIN - 1) + lane // LANES - lane % WIN + WIN - 1
+    wanted = step * (2 * WIN - 1) + lane % WIN - lane // LANES + WIN - 1
     pick = jnp.where((entry == wanted) & (step < 2 * WIN - 1), 1.0, 0.0).astype(BF)
     found = dot(parts, pick)
     found = found[0:8] + found[8:16] + found[16:24]
@@ -56,73 +63,94 @@
         strips[pl.ds(c, 8, stride=WIN), :] = found[:, c * LANES : (c + 1) * LANES]
 
 
-def bias_base(strips, queries):
-    tiles = []
-    for h in range(HEADS):
-        strip = strips[h * WIN : (h + 1) * WIN, :]
-        for r in range(WIN - queries // WIN, WIN):
-            by = (WIN - 1 - r) * WIN
-            tiles.append(pltpu.roll(strip, (LANES - by) % LANES, 1)[:, :TOK])
-    return jnp.concatenate(tiles, axis=0)
-
-
-def biases(strips, last_row, queries):
-    first = TOK - queries
-    base = bias_base(strips, queries)
-    shape = (HEADS * queries, TOK)
-    key = lax.broadcasted_iota(jnp.int32, shape, 1)
-    query = lax.broadcasted_iota(jnp.int32, shape, 0) % queries + first
-    rows_differ = (key // WIN >= SHIFT) != (query // WIN >= SHIFT)
-    cols_differ = (key % WIN >= SHIFT) != (query % WIN >= SHIFT)
-    row_pen = jnp.where(rows_differ, jnp.where(last_row, -100.0, 0.0).astype(F32), 0.0)
-    plain = base + row_pen
-    both = base + jnp.where(cols_differ, -100.0, row_pen)
-    return plain, both
-
-
-def head_masks():
-    lane = lax.broadcasted_iota(jnp.int32, (1, CHAN), 1)
-    return [
-        ((lane >= h * HEAD_DIM) & (lane < (h + 1) * HEAD_DIM)).astype(F32) for h in range(HEADS)
-    ]
-
-
-def attend(x, gain, wq, wk, wv, wp, bias_of, queries):
-    masks = head_masks()
-    low_masks = [m.astype(BF) for m in masks]
+def bias_fill(strips, bias, own_last, prev_last):
+    first_half = iota((WIN, LANES), 1) < TOK
+    for r in range(WIN):
+        by = 2 * LANES - (WIN - 1 - r) * WIN
+        tiles = []
+        for h in range(0, HEADS, 2):
+            even = strips[h * WIN : (h + 1) * WIN, :]
+            odd = strips[(h + 1) * WIN : (h + 2) * WIN, :]
+            tiles.append(
+                jnp.where(
+                    first_half,
+                    pltpu.roll(even, by % LANES, 1),
+                    pltpu.roll(odd, (by + TOK) % LANES, 1),
+                )
+            )
+        base = jnp.concatenate(tiles, axis=1)
+        shape = (WIN, QUERIES)
+        key, query = iota(shape, 0), iota(shape, 1) % TOK
+        rows_differ = (query // WIN >= SHIFT) != (r >= SHIFT)
+        cols_differ = (key >= SHIFT) != (query % WIN >= SHIFT)
+        rows = slice(r * WIN, (r + 1) * WIN)
+        for k, last in enumerate((own_last, prev_last)):
+            row_pen = jnp.where(rows_differ, jnp.where(last, -100.0, 0.0).astype(F32), 0.0)
+            bias[2 * k, rows] = base + row_pen
+            bias[2 * k + 1, rows] = base + jnp.where(cols_differ, -100.0, row_pen)
+
+
+def spread_heads(rows, cols):
+    row, col = iota((rows, cols), 0), iota((rows, cols), 1)
+    inside = row % DEPTH
+    wanted = row // DEPTH * CHAN + inside // PAD * HEAD_DIM + inside % PAD
+    return jnp.where((inside % PAD < HEAD_DIM) & (wanted == col), 1.0, 0.0).astype(BF)
+
+
+def attend(x, gain, w_in, w_out, bias_of):
     normed = layer_norm(x, gain)
-    if queries == TOK:
-        x_q, n_q = x, normed
-    else:
-        pick = lambda a: jnp.concatenate(
-            [a[g * TOK + TOK - queries : (g + 1) * TOK] for g in range(GROUP)], axis=0
-        )
-        x_q, n_q = pick(x), pick(normed)
-    q = (dot(n_q, wq) * HEAD_DIM ** (-0.5)).astype(BF)
-    k = dot(normed, wk).astype(BF)
-    v = dot(normed, wv).astype(BF)
-    mixed = []
-    for g in range(GROUP):
-        q_w = q[g * queries : (g + 1) * queries]
-        stacked = jnp.concatenate([q_w * low_masks[h] for h in range(HEADS)], axis=0)
-        scores = dot_t(stacked, k[g * TOK : (g + 1) * TOK]) + bias_of(g)
-        top = jnp.max(scores, axis=1, keepdims=True)
-        grown = jnp.exp(scores - top)
-        weights = (grown * (1.0 / jnp.sum(grown, axis=1, keepdims=True))).astype(BF)
-        wide = dot(weights, v[g * TOK : (g + 1) * TOK])
-        total = wide[:queries] * masks[0]
-        for h in range(1, HEADS):
-            total = total + wide[h * queries : (h + 1) * queries] * masks[h]
-        mixed.append(total)
-    mixed = jnp.concatenate(mixed, axis=0).astype(BF)
-    return (x_q + dot(mixed, wp)).astype(BF)
+    mixed = dot(w_in, normed)
+    q = mixed[0:DEPTH] * HEAD_DIM ** (-0.5)
+    k = mixed[DEPTH : 2 * DEPTH].T.astype(BF)
+    v = mixed[2 * DEPTH :].astype(BF)
+    low = iota((PAD, LANES), 1) < TOK
+    blank = jnp.zeros((PAD, LANES), F32)
+    joined = []
+    for pair in range(GROUP // 2):
+        lanes = slice(pair * LANES, (pair + 1) * LANES)
+        q_pair = q[:, lanes]
+        q_turn = pltpu.roll(q_pair, TOK, 1)
+        weights = []
+        for side in range(2):
+            g = 2 * pair + side
+            blocks = []
+            for h in range(HEADS):
+                part = slice(h * PAD, (h + 1) * PAD)
+                value = q_pair[part] if h % 2 == side else q_turn[part]
+                value = jnp.where(low if h % 2 == 0 else ~low, value, 0.0)
+                row = [blank] * (HEADS // 2)
+                row[h // 2] = value
+                blocks.append(jnp.concatenate(row, axis=1))
+            spread_q = jnp.concatenate(blocks, axis=0).astype(BF)
+            scores = dot(k[g * TOK : (g + 1) * TOK], spread_q) + bias_of(g)
+            top = jnp.max(scores, axis=0, keepdims=True)
+            grown = jnp.exp(scores - top)
+            weights.append((grown * (1.0 / jnp.sum(grown, axis=0, keepdims=True))).astype(BF))
+        rows = []
+        none = jnp.zeros((TOK, LANES), BF)
+        for j in range(HEADS // 2):
+            cut = slice(j * LANES, (j + 1) * LANES)
+            both = jnp.concatenate(
+                [
+                    jnp.concatenate([weights[0][:, cut], none], axis=1),
+                    jnp.concatenate([none, weights[1][:, cut]], axis=1),
+                ],
+                axis=0,
+            )
+            found = dot(v[2 * j * PAD : 2 * (j + 1) * PAD, lanes], both)
+            one, two = found[:, :LANES], found[:, LANES:]
+            rows.append(jnp.where(low, one[:PAD], pltpu.roll(two[:PAD], TOK, 1)))
+            rows.append(jnp.where(low, pltpu.roll(one[PAD:], TOK, 1), two[PAD:]))
+        joined.append(jnp.concatenate(rows, axis=0))
+    joined = jnp.concatenate(joined, axis=1).astype(BF)
+    return (x + dot(w_out, joined)).astype(BF)
 
 
 def feed(states, gain, wh, wo):
     flat = states.astype(F32)
     normed = layer_norm(flat, gain)
-    inner = jax.nn.gelu(dot(normed, wh)).astype(BF)
-    return (flat + dot_t(inner, wo)).astype(BF)
+    inner = jax.nn.gelu(dot(wh, normed)).astype(BF)
+    return (flat + dot(wo, inner)).astype(BF)
 
 
 def window_at(image, i, g, row):
@@ -131,7 +159,7 @@
 
 
 def group_at(image, i, row):
-    return jnp.concatenate([window_at(image, i, g, row) for g in range(GROUP)], axis=0)
+    return jnp.concatenate([window_at(image, i, g, row) for g in range(GROUP)], axis=0).T
 
 
 def plane_row(planes, row, channels):
@@ -144,8 +172,8 @@
 def block_kernel(
     keep, count, dests, slots, keep_row, pixels, table, gain_a, wqkv, wp, gain_m, wh, wo,
     restored, incoming,
-    planes, image, nxt_out, prv_out, nxt_buf, prv_buf, told, told_buf, weights, strips,
-    bias_own, bias_prev, first, rest, upper, result, active, outgoing, following, order,
+    planes, image, nxt_out, prv_out, nxt_buf, prv_buf, told, told_buf, w_in, w_out, w_hid, gains,
+    strips, bias, states, doubled, result, active, outgoing, following, order,
     halo_send, halo_recv, tile_send, tile_recv,
 ):
     bands = lax.axis_size("band")
@@ -211,11 +239,13 @@
         if r >= rows - SHIFT:
             prv_out[r - rows + SHIFT] = row.astype(BF)
         image[SHIFT + r] = row.T
-    for i in range(3):
-        weights[i] = wqkv[:, i * CHAN : (i + 1) * CHAN]
+    w_in[...] = dot_t(spread_heads(3 * DEPTH, 3 * CHAN), wqkv[...]).astype(BF)
+    w_out[...] = dot(spread_heads(DEPTH, CHAN), wp[...]).T.astype(BF)
+    w_hid[...] = wh[...].astype(F32).T.astype(BF)
+    gains[0] = jnp.broadcast_to(gain_a[...], (SIZE, channels)).T
+    gains[1] = jnp.broadcast_to(gain_m[...], (SIZE, channels)).T
     bias_strips(table, strips)
-    bias_own[0], bias_own[1] = biases(strips, me == bands - 1, TOK)
-    bias_prev[0], bias_prev[1] = biases(strips, me == 0, HALF)
+    bias_fill(strips, bias, me == bands - 1, me == 0)
 
     told[...] = jnp.zeros(told.shape, jnp.int32)
     told[:, 0:windows] = jnp.broadcast_to(keep_row[...], (8, windows))
@@ -250,21 +280,24 @@
 
     lax.fori_loop(0, windows, rank, following[0])
 
+    early = iota((channels, LANES), 1) < TOK
+
+    def attend_group(i, kind, row):
+        def edge(g):
+            return bias[2 * kind + (i * GROUP + g == windows - 1).astype(jnp.int32)]
+
+        return attend(group_at(image, i, row), gains[0], w_in[...], w_out[...], edge)
+
     def step(i, _):
-        def edge(g):
-            return bias_own[(i * GROUP + g == windows - 1).astype(jnp.int32)]
-
-        own = attend(
-            group_at(image, i, WIN), gain_a[...], weights[0], weights[1], weights[2], wp[...],
-            edge, TOK,
-        )
+        own = attend_group(i, 0, WIN)
+        states[i] = own
         wide = own.astype(F32)
-        for g in range(GROUP):
-            w = i * GROUP + g
-            upper[w] = own[g * TOK : g * TOK + HALF]
-            first[w] = own[g * TOK : (g + 1) * TOK, :LANES]
-            tail = wide[g * TOK : (g + 1) * TOK, LANES:]
-            rest[w] = jnp.concatenate([tail, jnp.zeros((TOK, 2 * LANES - CHAN), F32)], axis=1)
+        for pair in range(GROUP // 2):
+            block = wide[:, pair * LANES : (pair + 1) * LANES]
+            turned = pltpu.roll(block, TOK, 1)
+            w = i * GROUP + 2 * pair
+            doubled[w] = jnp.where(early, block, turned).astype(BF)
+            doubled[w + 1] = jnp.where(early, turned, block).astype(BF)
         return 0
 
     for c in range(halves):
@@ -276,8 +309,6 @@
             block = nxt_buf[r, :, c * LANES : (c + 1) * LANES].astype(F32)
             image[SHIFT + rows + r, c * LANES : (c + 1) * LANES, :] = block.T
         lax.fori_loop(c * groups // halves, (c + 1) * groups // halves, step, 0)
-
-    lane = lax.broadcasted_iota(jnp.int32, (TOK, LANES), 1)
 
     def pack(index, peer, j):
         t = jnp.int32(0)
@@ -292,12 +323,10 @@
         for p in range(TILE):
             position = t * TILE + p
             valid = live_tile & (position < live)
-            source = order[position]
-            value = first[source]
-            outgoing[index, p * TOK : (p + 1) * TOK] = jnp.where(valid, value, jnp.zeros_like(value))
-            halves_of.append(jnp.where(valid, rest[source], 0.0))
-        both = jnp.where(lane < TOK, halves_of[0], pltpu.roll(halves_of[1], TOK, 1))
-        outgoing[index, TILE * TOK :] = jnp.where(lane >= SLOT_LANE, slot, both).astype(BF)
+            value = doubled[order[position]]
+            halves_of.append(jnp.where(valid, value, jnp.zeros_like(value)))
+        outgoing[index, :channels] = jnp.where(early, halves_of[0], halves_of[1])
+        outgoing[index, DEPTH - 8 :] = jnp.full((8, LANES), slot, F32).astype(BF)
 
     def tile_copy(i):
         return pltpu.make_async_remote_copy(
@@ -323,41 +352,30 @@
     def blend(done, flags, w, row):
         cols_w = pl.ds(pl.multiple_of(w * WIN, WIN), WIN)
         chosen = active[flags, pl.ds(w, 1), :].reshape(1, 1, channels) > 0.5
-        value = done.reshape(SHIFT, WIN, CHAN)
         result[row : row + SHIFT, cols_w, :] = jnp.where(
-            chosen, value, image[SHIFT + row : 2 * SHIFT + row, cols_w, :]
+            chosen,
+            done.reshape(SHIFT, WIN, CHAN),
+            image[SHIFT + row : 2 * SHIFT + row, cols_w, :],
         )
-
-    def finish_own(i, _):
-        span_w = 2 * GROUP
-        states = jnp.concatenate([upper[i * span_w + g] for g in range(span_w)], axis=0)
-        done = feed(states, gain_m[...], wh[...], wo[...]).astype(F32)
-        for g in range(span_w):
-            blend(done[g * HALF : (g + 1) * HALF], 0, i * span_w + g, SHIFT)
-        return 0
-
-    lax.fori_loop(0, groups // 2, finish_own, 0)
 
     told_copy.wait()
     active[1] = spread(told_buf[...])
     prv_copy.wait()
     for r in range(SHIFT):
         image[r] = prv_buf[r].astype(F32).T
-
-    def finish_prev(i, _):
-        def edge(g):
-            return bias_prev[(i * GROUP + g == windows - 1).astype(jnp.int32)]
-
-        prev = attend(
-            group_at(image, i, 0), gain_a[...], weights[0], weights[1], weights[2], wp[...],
-            edge, HALF,
-        )
-        done = feed(prev, gain_m[...], wh[...], wo[...]).astype(F32)
+    upper = iota((channels, SIZE), 1) % TOK < HALF
+
+    def finish(i, _):
+        prev = attend_group(i, 1, 0)
+        mine = jnp.where(upper, states[i], prev)
+        done = feed(mine, gains[1], w_hid[...], wo[...]).astype(F32).T
         for g in range(GROUP):
-            blend(done[g * HALF : (g + 1) * HALF], 1, i * GROUP + g, 0)
+            w = i * GROUP + g
+            blend(done[g * TOK : g * TOK + HALF], 0, w, SHIFT)
+            blend(done[g * TOK + HALF : (g + 1) * TOK], 1, w, 0)
         return 0
 
-    lax.fori_loop(0, groups, finish_prev, 0)
+    lax.fori_loop(0, groups, finish, 0)
     for r in range(rows):
         row = pltpu.roll(result[r].T, SHIFT, 1)
         for h in range(halves):
@@ -377,19 +395,14 @@
 def place_kernel(incoming, work, planes):
     total = incoming.shape[0]
     channels = work.shape[0]
-    head = jnp.max(incoming[:, TILE * TOK : TILE * TOK + 16, :].astype(F32), axis=1)
-    lane = lax.broadcasted_iota(jnp.int32, (total, LANES), 1)
-    slot = jnp.max(jnp.where(lane >= SLOT_LANE, head, 0.0), axis=1, keepdims=True).astype(jnp.int32)
-    match = slot == lane
-    index = lax.broadcasted_iota(jnp.int32, (total, LANES), 0)
-    source = jnp.max(jnp.where(match, index, -1).astype(F32), axis=0, keepdims=True).astype(jnp.int32)
+    head = jnp.max(incoming[:, DEPTH - 8 :, :].astype(F32), axis=1)
+    slot = jnp.max(head, axis=1, keepdims=True).astype(jnp.int32)
+    match = slot == iota((total, LANES), 1)
+    source = jnp.where(match, iota((total, LANES), 0), -1).astype(F32)
+    source = jnp.max(source, axis=0, keepdims=True).astype(jnp.int32)
     for k in range(CAP):
         known = source[0, k] >= 0
-        t = jnp.maximum(source[0, k], 0)
-        main = incoming[t, : TILE * TOK].astype(F32)
-        tail = incoming[t, TILE * TOK :].astype(F32)
-        tails = jnp.concatenate([tail, pltpu.roll(tail, TOK, 1)], axis=0)
-        block = jnp.concatenate([main.T, tails.T[: channels - LANES]], axis=0)
+        block = incoming[jnp.maximum(source[0, k], 0), :channels].astype(F32)
         planes[pl.ds(k, channels, stride=CAP), :] = jnp.where(known, block, 0.0)
     work[...] = planes[...].reshape(channels, CAP, TILE * TOK).astype(BF)
 
@@ -406,7 +419,7 @@
     pairs = -(-tiles // bands)
     smem = pl.BlockSpec(memory_space=pltpu.SMEM)
     vmem = pl.BlockSpec(memory_space=pltpu.VMEM)
-    tile_shape = (bands * pairs, TILE * TOK + TOK, LANES)
+    tile_shape = (bands * pairs, DEPTH, LANES)
     restored, incoming = pl.pallas_call(
         block_kernel,
         out_shape=(
@@ -424,13 +437,14 @@
             pltpu.VMEM((SHIFT, channels, cols), BF),
             pltpu.VMEM((8, LANES), jnp.int32),
             pltpu.VMEM((8, LANES), jnp.int32),
-            pltpu.VMEM((3, channels, channels), BF),
+            pltpu.VMEM((3 * DEPTH, channels), BF),
+            pltpu.VMEM((channels, DEPTH), BF),
+            pltpu.VMEM((hidden_weight.shape[1], channels), BF),
+            pltpu.VMEM((2, channels, SIZE), F32),
             pltpu.VMEM((8 * WIN, LANES), F32),
-            pltpu.VMEM((2, HEADS * TOK, TOK), F32),
-            pltpu.VMEM((2, HEADS * HALF, TOK), F32),
-            pltpu.VMEM((windows, TOK, LANES), BF),
-            pltpu.VMEM((windows, TOK, LANES), F32),
-            pltpu.VMEM((windows, HALF, channels), BF),
+            pltpu.VMEM((4, TOK, QUERIES), F32),
+            pltpu.VMEM((windows // GROUP, channels, SIZE), BF),
+            pltpu.VMEM((windows, channels, LANES), BF),
             pltpu.VMEM((rows, cols, channels), F32),
             pltpu.VMEM((2, windows, channels), F32),
             pltpu.VMEM(tile_shape, BF),

time: 53.8 us -> 48.3 us (0.90)
  the two profiles are of different devices: /device:TPU:0 before, /device:TPU:11 now
where the time goes in v2:
time: 48.3 us; the launch traced here: 48.1 us
  Pallas kernels  44.8 us (93%)
  local copies, waits for them, and re-layouts  1.99 us (4%)
  between operations  1.3 us (3%)
    pallas_call x1, Pallas kernels, shards(): pl.pallas_call(block_kernel, out_shape=(jax.ShapeDtypeStruct((channels, r...  43.6 us
    unnamed x5, local copies, waits for them, and re-layouts  1.99 us
    pallas_call x1, Pallas kernels, shards(): pl.pallas_call(place_kernel, out_shape=jax.ShapeDtypeStruct((channels, CA...  1.17 us

profile of v2, /device:TPU:11, one launch (start us, length us, event | category | flops | bytes accessed | tf_op | source)
XLA Modules:
  0.0 48.1 jit_solution(8192836103887693866)
XLA Ops:
  1.3 43.6 %block.1 = (bf16[180,8,256]{2,1,0:T(8,128)(2,1)}, bf16[16,192,128]{2,1,0:T(8,128)(2,1)}) custom-call(s32[1,32]{1,0:T(1,128)} %keep_row.1, s32[1]{0:T(128)S(6)} %copy.15.count, s32[1,16]{1,0:T(1,128)} %dests.1, s32[1,16]{1,0:T(1,128)} %slots.1, s32[1,32]{1,0:T(1,128)} %keep_row.1, bf16[180,8,256]{2,1,0:T(8,128)(2,1)} %bitcast.9, f32[6,225]{1,0:T(8,128)} %bitcast.11, ...), custom_call_target="tpu_custom_call" | custom-call | flops 10000000000 | bytes 10000000 | tf_op jit(solution)/shard_map/block/pallas_call | solution.py:423
  44.9 0.0 copy-start
  44.9 1.1 %copy-done = bf16[16,192,128]{2,1,0:T(8,128)(2,1)S(1)} copy-done((bf16[16,192,128]{2,1,0:T(8,128)(2,1)S(1)}, bf16[16,192,128]{2,1,0:T(8,128)(2,1)}, u32[]{:S(2)}) %copy-start) | copy-done | bytes 786456
  46.1 0.0 copy-start.1
  46.1 1.2 %place.1 = bf16[180,8,128]{2,1,0:T(8,128)(2,1)} custom-call(bf16[16,192,128]{2,1,0:T(8,128)(2,1)S(1)} %copy-done), custom_call_target="tpu_custom_call" | custom-call | tf_op jit(solution)/shard_map/place/pallas_call | solution.py:468
  47.2 0.0 copy-done.1
  47.2 0.9 %copy.16 = bf16[8,256,180]{1,0,2:T(8,128)(2,1)} copy(bf16[8,256,180]{1,0,2:T(8,128)(2,1)S(1)} %bitcast.7) | data formatting | bytes 1474560
Async XLA Ops:
  44.9 1.1 %copy-start = (bf16[16,192,128]{2,1,0:T(8,128)(2,1)S(1)}, bf16[16,192,128]{2,1,0:T(8,128)(2,1)}, u32[]{:S(2)}) copy-start(bf16[16,192,128]{2,1,0:T(8,128)(2,1)} %get-tuple-element.5.incoming) | copy-start | bytes 2359300
  46.1 1.2 %copy-start.1 = (bf16[180,8,256]{2,1,0:T(8,128)(2,1)S(1)}, bf16[180,8,256]{2,1,0:T(8,128)(2,1)}, u32[]{:S(2)}) copy-start(bf16[180,8,256]{2,1,0:T(8,128)(2,1)} %get-tuple-element.4) | copy-start | bytes 2211844

commit v3 on v2

--- a/solution.py
+++ b/solution.py
@@ -14,8 +14,10 @@
 TOK = WIN * WIN
 HALF = TOK // 2
 HEAD_DIM = CHAN // HEADS
-GROUP = 16
+GROUP = 8
+WIDER = 2
 SIZE = GROUP * TOK
+PART = GROUP * WIN
 PAD = 32
 DEPTH = HEADS * PAD
 QUERIES = HEADS * TOK
@@ -30,7 +32,9 @@
 def layer_norm(values, gain):
     center = values - jnp.sum(values, axis=0, keepdims=True) * (1.0 / CHAN)
     spread = jnp.sum(center * center, axis=0, keepdims=True) * (1.0 / CHAN)
-    return (center * lax.rsqrt(spread + EPSILON) * gain).astype(BF)
+    scaled = center * lax.rsqrt(spread + EPSILON)
+    parts = [scaled[:, i : i + LANES] * gain for i in range(0, values.shape[1], LANES)]
+    return jnp.concatenate(parts, axis=1).astype(BF)
 
 
 def dot(a, b):
@@ -106,7 +110,7 @@
     low = iota((PAD, LANES), 1) < TOK
     blank = jnp.zeros((PAD, LANES), F32)
     joined = []
-    for pair in range(GROUP // 2):
+    for pair in range(x.shape[1] // LANES):
         lanes = slice(pair * LANES, (pair + 1) * LANES)
         q_pair = q[:, lanes]
         q_turn = pltpu.roll(q_pair, TOK, 1)
@@ -153,13 +157,13 @@
     return (flat + dot(wo, inner)).astype(BF)
 
 
-def window_at(image, i, g, row):
-    start = pl.multiple_of((i * GROUP + g) * WIN, WIN)
+def window_at(image, w, row):
+    start = pl.multiple_of(w * WIN, WIN)
     return image[row : row + WIN, pl.ds(start, WIN), :].reshape(TOK, CHAN)
 
 
-def group_at(image, i, row):
-    return jnp.concatenate([window_at(image, i, g, row) for g in range(GROUP)], axis=0).T
+def windows_at(image, start, number, row):
+    return jnp.concatenate([window_at(image, start + g, row) for g in range(number)], axis=0).T
 
 
 def plane_row(planes, row, channels):
@@ -170,8 +174,10 @@
 
 
 def block_kernel(
-    keep, count, dests, slots, keep_row, pixels, table, gain_a, wqkv, wp, gain_m, wh, wo,
+    count, keep_in, dests_in, slots_in, pixels_in, table_in, gain_a_in, wqkv_in, wp_in,
+    gain_m_in, wh_in, wo_in,
     restored, incoming,
+    keep, dests, slots, keep_row, pixels, table, gain_a, wqkv, wp, gain_m, wh, wo, loads,
     planes, image, nxt_out, prv_out, nxt_buf, prv_buf, told, told_buf, w_in, w_out, w_hid, gains,
     strips, bias, states, doubled, result, active, outgoing, following, order,
     halo_send, halo_recv, tile_send, tile_recv,
@@ -182,11 +188,27 @@
     channels, rows, cols = pixels.shape
     windows = cols // WIN
     groups = windows // GROUP
+    half = bands // 2
+    far = jnp.where(me < half, half, 0)
+    near = half - far
     halves = cols // LANES
     tiles = windows // TILE
     pairs = -(-tiles // bands)
     span = min(bands, tiles)
     mesh_id = pl.DeviceIdType.MESH
+    moves = [
+        pltpu.make_async_copy(source, target, loads.at[i])
+        for i, (source, target) in enumerate(
+            (
+                (pixels_in, pixels), (wqkv_in, wqkv), (wp_in, wp), (table_in, table),
+                (gain_a_in, gain_a), (gain_m_in, gain_m), (wh_in, wh), (wo_in, wo),
+                (keep_in, keep_row), (keep_in, keep), (dests_in, dests),
+                (slots_in, slots),
+            )
+        )
+    ]
+    for move in moves:
+        move.start()
 
     barrier = pltpu.get_barrier_semaphore()
 
@@ -197,18 +219,25 @@
 
     lax.fori_loop(1, bands, greet, 0)
 
+    moves[0].wait()
     for h in range(halves):
         part = pixels[:, :, h * LANES : (h + 1) * LANES].astype(F32)
         planes[h] = part.reshape(channels * rows, LANES)
-    for r in range(SHIFT):
-        nxt_out[r] = pltpu.roll(plane_row(planes, r, channels), cols - SHIFT, 1).astype(BF)
+    front = iota((channels, LANES), 1) < PART
+    for r in range(0, SHIFT, 2):
+        one = pltpu.roll(plane_row(planes, r, channels), cols - SHIFT, 1)
+        two = pltpu.roll(plane_row(planes, r + 1, channels), cols - SHIFT, 1)
+        lanes = slice(r * PART, (r + 2) * PART)
+        for h in range(halves):
+            a, b = one[:, h * LANES : (h + 1) * LANES], two[:, h * LANES : (h + 1) * LANES]
+            nxt_out[2 * h, :, lanes] = jnp.where(front, a, pltpu.roll(b, PART, 1)).astype(BF)
+            nxt_out[2 * h + 1, :, lanes] = jnp.where(front, pltpu.roll(a, PART, 1), b).astype(BF)
     pl.semaphore_wait(barrier, bands - 1)
 
     def nxt_copy(c):
-        part = pl.ds(pl.multiple_of(c * LANES, LANES), LANES)
         return pltpu.make_async_remote_copy(
-            src_ref=nxt_out.at[:, :, part],
-            dst_ref=nxt_buf.at[:, :, part],
+            src_ref=nxt_out.at[c],
+            dst_ref=nxt_buf.at[c],
             send_sem=halo_send.at[c],
             recv_sem=halo_recv.at[c],
             device_id={"band": left},
@@ -218,20 +247,20 @@
     prv_copy = pltpu.make_async_remote_copy(
         src_ref=prv_out,
         dst_ref=prv_buf,
-        send_sem=halo_send.at[halves],
-        recv_sem=halo_recv.at[halves],
+        send_sem=halo_send.at[groups],
+        recv_sem=halo_recv.at[groups],
         device_id={"band": right},
         device_id_type=mesh_id,
     )
     told_copy = pltpu.make_async_remote_copy(
         src_ref=told,
         dst_ref=told_buf,
-        send_sem=halo_send.at[halves + 1],
-        recv_sem=halo_recv.at[halves + 1],
+        send_sem=halo_send.at[groups + 1],
+        recv_sem=halo_recv.at[groups + 1],
         device_id={"band": right},
         device_id_type=mesh_id,
     )
-    for c in range(halves):
+    for c in range(groups):
         nxt_copy(c).start()
 
     for r in range(rows):
@@ -239,11 +268,14 @@
         if r >= rows - SHIFT:
             prv_out[r - rows + SHIFT] = row.astype(BF)
         image[SHIFT + r] = row.T
+    prv_copy.start()
+    for move in moves[1:]:
+        move.wait()
     w_in[...] = dot_t(spread_heads(3 * DEPTH, 3 * CHAN), wqkv[...]).astype(BF)
     w_out[...] = dot(spread_heads(DEPTH, CHAN), wp[...]).T.astype(BF)
     w_hid[...] = wh[...].astype(F32).T.astype(BF)
-    gains[0] = jnp.broadcast_to(gain_a[...], (SIZE, channels)).T
-    gains[1] = jnp.broadcast_to(gain_m[...], (SIZE, channels)).T
+    gains[0] = jnp.broadcast_to(gain_a[...], (LANES, channels)).T
+    gains[1] = jnp.broadcast_to(gain_m[...], (LANES, channels)).T
     bias_strips(table, strips)
     bias_fill(strips, bias, me == bands - 1, me == 0)
 
@@ -263,6 +295,7 @@
         chosen = jnp.where(diagonal, jnp.broadcast_to(flags[0:1].astype(F32), own_lane), 0.0)
         return dot(chosen.astype(BF), jnp.ones((LANES, channels), BF))
 
+    told_copy.start()
     active[0] = spread(told[...])
 
     following[windows] = jnp.int32(windows)
@@ -280,35 +313,35 @@
 
     lax.fori_loop(0, windows, rank, following[0])
 
-    early = iota((channels, LANES), 1) < TOK
-
-    def attend_group(i, kind, row):
+    padded = channels + 4
+    early = iota((padded, LANES), 1) < TOK
+
+    def attend_windows(start, number, kind, row):
         def edge(g):
-            return bias[2 * kind + (i * GROUP + g == windows - 1).astype(jnp.int32)]
-
-        return attend(group_at(image, i, row), gains[0], w_in[...], w_out[...], edge)
-
-    def step(i, _):
-        own = attend_group(i, 0, WIN)
-        states[i] = own
-        wide = own.astype(F32)
+            return bias[2 * kind + (start + g == windows - 1).astype(jnp.int32)]
+
+        x = windows_at(image, start, number, row)
+        return attend(x, gains[0], w_in[...], w_out[...], edge)
+
+    def step(c, _):
+        nxt_copy(c).wait()
+        block = nxt_buf[c].astype(F32).T
+        cut = pl.ds(pl.multiple_of(c * PART, PART), PART)
+        for r in range(SHIFT):
+            image[SHIFT + rows + r, cut, :] = block[r * PART : (r + 1) * PART]
+        own = attend_windows(c * GROUP, GROUP, 0, WIN)
+        states[c] = own
+        wide = jnp.concatenate([own.astype(F32), jnp.zeros((4, SIZE), F32)], axis=0)
         for pair in range(GROUP // 2):
-            block = wide[:, pair * LANES : (pair + 1) * LANES]
-            turned = pltpu.roll(block, TOK, 1)
-            w = i * GROUP + 2 * pair
-            doubled[w] = jnp.where(early, block, turned).astype(BF)
-            doubled[w + 1] = jnp.where(early, turned, block).astype(BF)
+            both = wide[:, pair * LANES : (pair + 1) * LANES]
+            turned = pltpu.roll(both, TOK, 1)
+            w = c * GROUP + 2 * pair
+            doubled[w] = jnp.where(early, both, turned).astype(BF)
+            doubled[w + 1] = jnp.where(early, turned, both).astype(BF)
         return 0
 
-    for c in range(halves):
-        nxt_copy(c).wait()
-        if c == halves - 1:
-            told_copy.start()
-            prv_copy.start()
-        for r in range(SHIFT):
-            block = nxt_buf[r, :, c * LANES : (c + 1) * LANES].astype(F32)
-            image[SHIFT + rows + r, c * LANES : (c + 1) * LANES, :] = block.T
-        lax.fori_loop(c * groups // halves, (c + 1) * groups // halves, step, 0)
+    lax.fori_loop(0, groups, step, 0)
+    slot_row = iota((padded, LANES), 0) >= channels
 
     def pack(index, peer, j):
         t = jnp.int32(0)
@@ -325,29 +358,35 @@
             valid = live_tile & (position < live)
             value = doubled[order[position]]
             halves_of.append(jnp.where(valid, value, jnp.zeros_like(value)))
-        outgoing[index, :channels] = jnp.where(early, halves_of[0], halves_of[1])
-        outgoing[index, DEPTH - 8 :] = jnp.full((8, LANES), slot, F32).astype(BF)
-
-    def tile_copy(i):
+        value = jnp.where(early, halves_of[0], halves_of[1])
+        outgoing[index] = jnp.where(slot_row, jnp.full((padded, LANES), slot, F32).astype(BF), value)
+
+    def peer_of(n):
+        return jnp.where(
+            n < half, far + lax.rem(me + n, half), near + lax.rem(me - near + n - half + 1, half)
+        )
+
+    def tile_copy(n):
         return pltpu.make_async_remote_copy(
-            src_ref=outgoing.at[pl.ds(i * pairs, pairs)],
+            src_ref=outgoing.at[pl.ds(n * pairs, pairs)],
             dst_ref=incoming.at[pl.ds(me * pairs, pairs)],
-            send_sem=tile_send.at[i],
-            recv_sem=tile_recv.at[i],
-            device_id={"band": lax.rem(me + i, bands)},
+            send_sem=tile_send.at[n],
+            recv_sem=tile_recv.at[n],
+            device_id={"band": peer_of(n)},
             device_id_type=mesh_id,
         )
 
-    def dispatch(i, _):
+    def dispatch(n, _):
         for j in range(pairs):
-            pack(i * pairs + j, lax.rem(me + i, bands), j)
-        tile_copy(i).start()
+            pack(n * pairs + j, peer_of(n), j)
+        tile_copy(n).start()
         return 0
 
-    lax.fori_loop(1, bands, dispatch, 0)
+    lax.fori_loop(0, bands - 1, dispatch, 0)
+    kept_here = (bands - 1) * pairs
     for j in range(pairs):
-        pack(j, me, j)
-    incoming[pl.ds(me * pairs, pairs)] = outgoing[0:pairs]
+        pack(kept_here + j, me, j)
+    incoming[pl.ds(me * pairs, pairs)] = outgoing[kept_here : kept_here + pairs]
 
     def blend(done, flags, w, row):
         cols_w = pl.ds(pl.multiple_of(w * WIN, WIN), WIN)
@@ -363,19 +402,21 @@
     prv_copy.wait()
     for r in range(SHIFT):
         image[r] = prv_buf[r].astype(F32).T
-    upper = iota((channels, SIZE), 1) % TOK < HALF
+    upper = iota((channels, WIDER * SIZE), 1) % TOK < HALF
 
     def finish(i, _):
-        prev = attend_group(i, 1, 0)
-        mine = jnp.where(upper, states[i], prev)
+        number = WIDER * GROUP
+        prev = attend_windows(i * number, number, 1, 0)
+        own = jnp.concatenate([states[i * WIDER + k] for k in range(WIDER)], axis=1)
+        mine = jnp.where(upper, own, prev)
         done = feed(mine, gains[1], w_hid[...], wo[...]).astype(F32).T
-        for g in range(GROUP):
-            w = i * GROUP + g
+        for g in range(number):
+            w = i * number + g
             blend(done[g * TOK : g * TOK + HALF], 0, w, SHIFT)
             blend(done[g * TOK + HALF : (g + 1) * TOK], 1, w, 0)
         return 0
 
-    lax.fori_loop(0, groups, finish, 0)
+    lax.fori_loop(0, groups // WIDER, finish, 0)
     for r in range(rows):
         row = pltpu.roll(result[r].T, SHIFT, 1)
         for h in range(halves):
@@ -389,22 +430,26 @@
         tile_copy(i).wait()
         return 0
 
-    lax.fori_loop(1, bands, collect, 0)
-
-
-def place_kernel(incoming, work, planes):
-    total = incoming.shape[0]
+    lax.fori_loop(0, bands - 1, collect, 0)
+
+
+def place_kernel(incoming, restored, restored_out, work, planes, sem):
+    total, padded, _ = incoming.shape
     channels = work.shape[0]
-    head = jnp.max(incoming[:, DEPTH - 8 :, :].astype(F32), axis=1)
+    move = pltpu.make_async_copy(restored, restored_out, sem)
+    move.start()
+    head = incoming[:, padded - 8 :, :].astype(F32)
+    head = jnp.max(jnp.where(iota(head.shape, 1) >= 4, head, 0.0), axis=1)
     slot = jnp.max(head, axis=1, keepdims=True).astype(jnp.int32)
     match = slot == iota((total, LANES), 1)
     source = jnp.where(match, iota((total, LANES), 0), -1).astype(F32)
     source = jnp.max(source, axis=0, keepdims=True).astype(jnp.int32)
     for k in range(CAP):
         known = source[0, k] >= 0
-        block = incoming[jnp.maximum(source[0, k], 0), :channels].astype(F32)
+        block = incoming[jnp.maximum(source[0, k], 0)].astype(F32)[:channels]
         planes[pl.ds(k, channels, stride=CAP), :] = jnp.where(known, block, 0.0)
     work[...] = planes[...].reshape(channels, CAP, TILE * TOK).astype(BF)
+    move.wait()
 
 
 def shards(
@@ -419,61 +464,76 @@
     pairs = -(-tiles // bands)
     smem = pl.BlockSpec(memory_space=pltpu.SMEM)
     vmem = pl.BlockSpec(memory_space=pltpu.VMEM)
-    tile_shape = (bands * pairs, DEPTH, LANES)
+    tile_shape = (bands * pairs, channels + 4, LANES)
+    groups = windows // GROUP
+    nxt_shape = (groups, channels, SHIFT * PART)
+    operands = (
+        keep_mask, plan_dest, plan_slot, jnp.transpose(pixels, (2, 0, 1)),
+        bias_table.T, gain_attn[None], qkv_weight, proj_weight, gain_mlp[None], hidden_weight,
+        output_weight.T,
+    )
     restored, incoming = pl.pallas_call(
         block_kernel,
         out_shape=(
             jax.ShapeDtypeStruct((channels, rows, cols), BF),
             jax.ShapeDtypeStruct(tile_shape, BF),
         ),
-        in_specs=[smem] * 4 + [vmem] * 9,
+        in_specs=[smem] + [pl.BlockSpec(memory_space=pltpu.HBM)] * len(operands),
         out_specs=(vmem, vmem),
         scratch_shapes=[
+            pltpu.SMEM(operands[0].shape, jnp.int32),
+            pltpu.SMEM(operands[1].shape, jnp.int32),
+            pltpu.SMEM(operands[2].shape, jnp.int32),
+            pltpu.VMEM(operands[0].shape, jnp.int32),
+            *(pltpu.VMEM(operand.shape, operand.dtype) for operand in operands[3:]),
+            pltpu.SemaphoreType.DMA((len(operands) + 1,)),
             pltpu.VMEM((halves, channels * rows, LANES), F32),
             pltpu.VMEM((rows + 2 * SHIFT, cols, channels), F32),
+            pltpu.VMEM(nxt_shape, BF),
             pltpu.VMEM((SHIFT, channels, cols), BF),
-            pltpu.VMEM((SHIFT, channels, cols), BF),
-            pltpu.VMEM((SHIFT, channels, cols), BF),
+            pltpu.VMEM(nxt_shape, BF),
             pltpu.VMEM((SHIFT, channels, cols), BF),
             pltpu.VMEM((8, LANES), jnp.int32),
             pltpu.VMEM((8, LANES), jnp.int32),
             pltpu.VMEM((3 * DEPTH, channels), BF),
             pltpu.VMEM((channels, DEPTH), BF),
             pltpu.VMEM((hidden_weight.shape[1], channels), BF),
-            pltpu.VMEM((2, channels, SIZE), F32),
+            pltpu.VMEM((2, channels, LANES), F32),
             pltpu.VMEM((8 * WIN, LANES), F32),
             pltpu.VMEM((4, TOK, QUERIES), F32),
-            pltpu.VMEM((windows // GROUP, channels, SIZE), BF),
-            pltpu.VMEM((windows, channels, LANES), BF),
+            pltpu.VMEM((groups, channels, SIZE), BF),
+            pltpu.VMEM((windows, channels + 4, LANES), BF),
             pltpu.VMEM((rows, cols, channels), F32),
             pltpu.VMEM((2, windows, channels), F32),
             pltpu.VMEM(tile_shape, BF),
             pltpu.SMEM((windows + 1,), jnp.int32),
             pltpu.SMEM((windows,), jnp.int32),
-            pltpu.SemaphoreType.DMA((halves + 2,)),
-            pltpu.SemaphoreType.DMA((halves + 2,)),
+            pltpu.SemaphoreType.DMA((groups + 2,)),
+            pltpu.SemaphoreType.DMA((groups + 2,)),
             pltpu.SemaphoreType.DMA((bands,)),
             pltpu.SemaphoreType.DMA((bands,)),
         ],
         compiler_params=pltpu.CompilerParams(
-            vmem_limit_bytes=63 * 1024 * 1024, collective_id=0, has_side_effects=True
+            vmem_limit_bytes=40 * 1024 * 1024, collective_id=0, has_side_effects=True
         ),
         cost_estimate=pl.CostEstimate(flops=10**10, bytes_accessed=10**7, transcendentals=10**6),
         name="block",
-    )(
-        keep_mask, band_counts, plan_dest, plan_slot, keep_mask, jnp.transpose(pixels, (2, 0, 1)),
-        bias_table.T, gain_attn[None], qkv_weight, proj_weight, gain_mlp[None], hidden_weight,
-        output_weight.T,
-    )
-    work = pl.pallas_call(
+    )(band_counts, *(pltpu.with_memory_space_constraint(value, pltpu.HBM) for value in operands))
+    restored, work = pl.pallas_call(
         place_kernel,
-        out_shape=jax.ShapeDtypeStruct((channels, CAP, TILE * TOK), BF),
-        in_specs=[vmem],
-        out_specs=vmem,
-        scratch_shapes=[pltpu.VMEM((channels * CAP, TILE * TOK), F32)],
+        out_shape=(
+            jax.ShapeDtypeStruct((channels, rows, cols), BF),
+            jax.ShapeDtypeStruct((channels, CAP, TILE * TOK), BF),
+        ),
+        in_specs=[vmem, vmem],
+        out_specs=(pl.BlockSpec(memory_space=pl.ANY), vmem),
+        scratch_shapes=[
+            pltpu.VMEM((channels * CAP, TILE * TOK), F32),
+            pltpu.SemaphoreType.DMA,
+        ],
         compiler_params=pltpu.CompilerParams(vmem_limit_bytes=16 * 1024 * 1024),
         name="place",
-    )(incoming)
+    )(incoming, restored)
     return jnp.transpose(restored, (1, 2, 0)), jnp.transpose(work, (1, 2, 0))
 
 

time: 48.3 us -> 45.2 us (0.936)
  the two profiles are of different devices: /device:TPU:11 before, /device:TPU:0 now
where the time goes in v3:
time: 45.2 us; the launch traced here: 45.1 us
  Pallas kernels  43.8 us (97%)
  between operations  1.29 us (3%)
    pallas_call x1, Pallas kernels, shards(): pl.pallas_call(block_kernel, out_shape=(jax.ShapeDtypeStruct((channels, r...  41.9 us
    pallas_call x1, Pallas kernels, shards(): pl.pallas_call(place_kernel, out_shape=(jax.ShapeDtypeStruct((channels, r...  1.9 us

profile of v3, /device:TPU:0, one launch (start us, length us, event | category | flops | bytes accessed | tf_op | source)
XLA Modules:
  0.0 45.1 jit_solution(13525219198759173536)
XLA Ops:
  1.3 41.9 %block.1 = (bf16[180,8,256]{2,1,0:T(8,128)(2,1)S(1)}, bf16[16,184,128]{2,1,0:T(8,128)(2,1)S(1)}) custom-call(s32[1]{0:T(128)S(6)} %copy.14.count, s32[1,32]{1,0:T(1,128)} %keep_in.1, s32[1,16]{1,0:T(1,128)} %dests_in.1, s32[1,16]{1,0:T(1,128)} %slots_in.1, bf16[180,8,256]{2,1,0:T(8,128)(2,1)} %bitcast.7, f32[6,225]{1,0:T(8,128)} %bitcast.11, ...), custom_call_target="tpu_custom_call" | custom-call | flops 10000000000 | bytes 10000000 | tf_op jit(solution)/shard_map/block/pallas_call | solution.py:475
  43.2 1.9 %place.1 = (bf16[180,8,256]{2,1,0:T(8,128)(2,1)}, bf16[180,8,128]{2,1,0:T(8,128)(2,1)}) custom-call(bf16[16,184,128]{2,1,0:T(8,128)(2,1)S(1)} %get-tuple-element.6.incoming, bf16[180,8,256]{2,1,0:T(8,128)(2,1)S(1)} %get-tuple-element.7.restored), custom_call_target="tpu_custom_call" | custom-call | tf_op jit(solution)/shard_map/place/pallas_call | solution.py:522

commit v4 on v3

--- a/solution.py
+++ b/solution.py
@@ -189,6 +189,7 @@
     windows = cols // WIN
     groups = windows // GROUP
     half = bands // 2
+    fourth = half // 2
     far = jnp.where(me < half, half, 0)
     near = half - far
     halves = cols // LANES
@@ -244,22 +245,32 @@
             device_id_type=mesh_id,
         )
 
-    prv_copy = pltpu.make_async_remote_copy(
-        src_ref=prv_out,
-        dst_ref=prv_buf,
+    odd = lax.rem(me, 2) == 1
+    fold = SHIFT // 2
+
+    def prv_send(part, source, start, device, mark):
+        first = part * fold
+        return pltpu.make_async_remote_copy(
+            src_ref=source.at[first : first + fold],
+            dst_ref=prv_buf.at[start + first : start + first + fold],
+            send_sem=halo_send.at[groups + 1 + 2 * mark + part],
+            recv_sem=halo_recv.at[groups + 1 + 2 * mark + part],
+            device_id={"band": device},
+            device_id_type=mesh_id,
+        )
+
+    direct = [prv_send(part, prv_out, 0, right, 0) for part in range(2)]
+    relay = [prv_send(part, prv_out, SHIFT, lax.rem(me + 2, bands), 1) for part in range(2)]
+    held = prv_buf.at[SHIFT:]
+    forward = [prv_send(part, held, 0, left, 0) for part in range(2)]
+    told_copy = pltpu.make_async_remote_copy(
+        src_ref=told,
+        dst_ref=told_buf,
         send_sem=halo_send.at[groups],
         recv_sem=halo_recv.at[groups],
         device_id={"band": right},
         device_id_type=mesh_id,
     )
-    told_copy = pltpu.make_async_remote_copy(
-        src_ref=told,
-        dst_ref=told_buf,
-        send_sem=halo_send.at[groups + 1],
-        recv_sem=halo_recv.at[groups + 1],
-        device_id={"band": right},
-        device_id_type=mesh_id,
-    )
     for c in range(groups):
         nxt_copy(c).start()
 
@@ -268,7 +279,11 @@
         if r >= rows - SHIFT:
             prv_out[r - rows + SHIFT] = row.astype(BF)
         image[SHIFT + r] = row.T
-    prv_copy.start()
+    @pl.when(odd)
+    def _():
+        for part in range(2):
+            relay[part].start()
+
     for move in moves[1:]:
         move.wait()
     w_in[...] = dot_t(spread_heads(3 * DEPTH, 3 * CHAN), wqkv[...]).astype(BF)
@@ -325,6 +340,17 @@
 
     def step(c, _):
         nxt_copy(c).wait()
+
+        @pl.when((c == groups - 1) & odd)
+        def _():
+            relay[0].wait()
+            forward[0].start()
+
+        @pl.when((c == groups - 1) & ~odd)
+        def _():
+            for part in range(2):
+                direct[part].start()
+
         block = nxt_buf[c].astype(F32).T
         cut = pl.ds(pl.multiple_of(c * PART, PART), PART)
         for r in range(SHIFT):
@@ -341,6 +367,12 @@
         return 0
 
     lax.fori_loop(0, groups, step, 0)
+
+    @pl.when(odd)
+    def _():
+        relay[1].wait()
+        forward[1].start()
+
     slot_row = iota((padded, LANES), 0) >= channels
 
     def pack(index, peer, j):
@@ -362,9 +394,12 @@
         outgoing[index] = jnp.where(slot_row, jnp.full((padded, LANES), slot, F32).astype(BF), value)
 
     def peer_of(n):
-        return jnp.where(
-            n < half, far + lax.rem(me + n, half), near + lax.rem(me - near + n - half + 1, half)
-        )
+        away = n >= half
+        m = jnp.where(away, n - half + 1, n)
+        cross = (m >= fourth).astype(jnp.int32)
+        row = lax.rem(lax.div(lax.rem(me, half), 2) + m, fourth)
+        side = lax.rem(lax.rem(me, 2) + cross, 2)
+        return jnp.where(away, near, far) + 2 * row + side
 
     def tile_copy(n):
         return pltpu.make_async_remote_copy(
@@ -399,7 +434,19 @@
 
     told_copy.wait()
     active[1] = spread(told_buf[...])
-    prv_copy.wait()
+    for part in range(2):
+        direct[part].wait_recv()
+
+    @pl.when(~odd)
+    def _():
+        for part in range(2):
+            direct[part].wait_send()
+
+    @pl.when(odd)
+    def _():
+        for part in range(2):
+            forward[part].wait_send()
+
     for r in range(SHIFT):
         image[r] = prv_buf[r].astype(F32).T
     upper = iota((channels, WIDER * SIZE), 1) % TOK < HALF
@@ -492,7 +539,7 @@
             pltpu.VMEM(nxt_shape, BF),
             pltpu.VMEM((SHIFT, channels, cols), BF),
             pltpu.VMEM(nxt_shape, BF),
-            pltpu.VMEM((SHIFT, channels, cols), BF),
+            pltpu.VMEM((2 * SHIFT, channels, cols), BF),
             pltpu.VMEM((8, LANES), jnp.int32),
             pltpu.VMEM((8, LANES), jnp.int32),
             pltpu.VMEM((3 * DEPTH, channels), BF),
@@ -508,8 +555,8 @@
             pltpu.VMEM(tile_shape, BF),
             pltpu.SMEM((windows + 1,), jnp.int32),
             pltpu.SMEM((windows,), jnp.int32),
-            pltpu.SemaphoreType.DMA((groups + 2,)),
-            pltpu.SemaphoreType.DMA((groups + 2,)),
+            pltpu.SemaphoreType.DMA((groups + 5,)),
+            pltpu.SemaphoreType.DMA((groups + 5,)),
             pltpu.SemaphoreType.DMA((bands,)),
             pltpu.SemaphoreType.DMA((bands,)),
         ],

time: 45.2 us -> 42.2 us (0.934)
  Pallas kernels: 43.8 us -> 40.7 us
    pallas_call x1, Pallas kernels: 41.9 us -> 38.8 us  [shards(): pl.pallas_call(block_kernel, out_shape=(jax.ShapeDtypeStruct((channels, r...]
where the time goes in v4:
time: 42.2 us; the launch traced here: 42 us
  Pallas kernels  40.7 us (96%)
  between operations  1.29 us (3%)
    pallas_call x1, Pallas kernels, shards(): pl.pallas_call(block_kernel, out_shape=(jax.ShapeDtypeStruct((channels, r...  38.8 us
    pallas_call x1, Pallas kernels, shards(): pl.pallas_call(place_kernel, out_shape=(jax.ShapeDtypeStruct((channels, r...  1.9 us

profile of v4, /device:TPU:0, one launch (start us, length us, event | category | flops | bytes accessed | tf_op | source)
XLA Modules:
  0.0 42.0 jit_solution(13287219235418372675)
XLA Ops:
  1.3 38.8 %block.1 = (bf16[180,8,256]{2,1,0:T(8,128)(2,1)S(1)}, bf16[16,184,128]{2,1,0:T(8,128)(2,1)S(1)}) custom-call(s32[1]{0:T(128)S(6)} %copy.14.count, s32[1,32]{1,0:T(1,128)} %keep_in.1, s32[1,16]{1,0:T(1,128)} %dests_in.1, s32[1,16]{1,0:T(1,128)} %slots_in.1, bf16[180,8,256]{2,1,0:T(8,128)(2,1)} %bitcast.7, f32[6,225]{1,0:T(8,128)} %bitcast.11, ...), custom_call_target="tpu_custom_call" | custom-call | flops 10000000000 | bytes 10000000 | tf_op jit(solution)/shard_map/block/pallas_call | solution.py:522
  40.1 1.9 %place.1 = (bf16[180,8,256]{2,1,0:T(8,128)(2,1)}, bf16[180,8,128]{2,1,0:T(8,128)(2,1)}) custom-call(bf16[16,184,128]{2,1,0:T(8,128)(2,1)S(1)} %get-tuple-element.6.incoming, bf16[180,8,256]{2,1,0:T(8,128)(2,1)S(1)} %get-tuple-element.7.restored), custom_call_target="tpu_custom_call" | custom-call | tf_op jit(solution)/shard_map/place/pallas_call | solution.py:569

commit v5 on v4

--- a/solution.py
+++ b/solution.py
@@ -157,13 +157,40 @@
     return (flat + dot(wo, inner)).astype(BF)
 
 
-def window_at(image, w, row):
-    start = pl.multiple_of(w * WIN, WIN)
-    return image[row : row + WIN, pl.ds(start, WIN), :].reshape(TOK, CHAN)
-
-
-def windows_at(image, start, number, row):
-    return jnp.concatenate([window_at(image, start + g, row) for g in range(number)], axis=0).T
+def window_order():
+    shape = (SIZE, SIZE)
+    source, target = iota(shape, 0), iota(shape, 1)
+    col = source % PART
+    row = source // (SIZE // 2) * SHIFT + source % (SIZE // 2) // PART
+    wanted = col // WIN * TOK + row * WIN + col % WIN
+    return jnp.where(wanted == target, 1.0, 0.0).astype(BF)
+
+
+def ranks(flags, windows):
+    kept = flags.astype(F32)
+    other = jnp.where(iota(flags.shape, 1) < windows, 1.0, 0.0) - kept
+    tri = (LANES, LANES)
+    before = jnp.where(iota(tri, 0) < iota(tri, 1), 1.0, 0.0).astype(BF)
+    total = dot(kept.astype(BF), jnp.ones(tri, BF))
+    ahead = dot(kept.astype(BF), before)
+    return jnp.where(flags == 1, ahead, total + dot(other.astype(BF), before))
+
+
+def column_order(rank, cols):
+    shape = (cols, LANES)
+    shifted = (iota(shape, 0) + cols - SHIFT) % cols
+    spread = jnp.where(shifted // WIN == iota(shape, 1), jnp.broadcast_to(rank[0:1], shape), 0.0)
+    first = dot(spread.astype(BF), jnp.ones((LANES, cols), BF))
+    shape = (cols, cols)
+    inside = ((iota(shape, 0) + cols - SHIFT) % WIN).astype(F32)
+    wanted = first * WIN + inside
+    return jnp.where(wanted == iota(shape, 1).astype(F32), 1.0, 0.0).astype(BF)
+
+
+def swap_parts(one, two):
+    front = iota(one.shape, 1) < PART
+    even = jnp.where(front, one, pltpu.roll(two, PART, 1))
+    return even, jnp.where(front, pltpu.roll(one, PART, 1), two)
 
 
 def plane_row(planes, row, channels):
@@ -178,8 +205,8 @@
     gain_m_in, wh_in, wo_in,
     restored, incoming,
     keep, dests, slots, keep_row, pixels, table, gain_a, wqkv, wp, gain_m, wh, wo, loads,
-    planes, image, nxt_out, prv_out, nxt_buf, prv_buf, told, told_buf, w_in, w_out, w_hid, gains,
-    strips, bias, states, doubled, result, active, outgoing, following, order,
+    planes, nxt_out, prv_out, nxt_buf, prv_buf, told, told_buf, w_in, w_out, w_hid, gains,
+    strips, bias, order, columns, states, origin, done_rows, packed, outgoing,
     halo_send, halo_recv, tile_send, tile_recv,
 ):
     bands = lax.axis_size("band")
@@ -201,10 +228,9 @@
         pltpu.make_async_copy(source, target, loads.at[i])
         for i, (source, target) in enumerate(
             (
-                (pixels_in, pixels), (wqkv_in, wqkv), (wp_in, wp), (table_in, table),
-                (gain_a_in, gain_a), (gain_m_in, gain_m), (wh_in, wh), (wo_in, wo),
-                (keep_in, keep_row), (keep_in, keep), (dests_in, dests),
-                (slots_in, slots),
+                (keep_in, keep_row), (pixels_in, pixels), (wqkv_in, wqkv), (wp_in, wp),
+                (table_in, table), (gain_a_in, gain_a), (gain_m_in, gain_m), (wh_in, wh),
+                (wo_in, wo), (keep_in, keep), (dests_in, dests), (slots_in, slots),
             )
         )
     ]
@@ -220,20 +246,16 @@
 
     lax.fori_loop(1, bands, greet, 0)
 
+    live = count[0]
     moves[0].wait()
-    for h in range(halves):
-        part = pixels[:, :, h * LANES : (h + 1) * LANES].astype(F32)
-        planes[h] = part.reshape(channels * rows, LANES)
-    front = iota((channels, LANES), 1) < PART
-    for r in range(0, SHIFT, 2):
-        one = pltpu.roll(plane_row(planes, r, channels), cols - SHIFT, 1)
-        two = pltpu.roll(plane_row(planes, r + 1, channels), cols - SHIFT, 1)
-        lanes = slice(r * PART, (r + 2) * PART)
-        for h in range(halves):
-            a, b = one[:, h * LANES : (h + 1) * LANES], two[:, h * LANES : (h + 1) * LANES]
-            nxt_out[2 * h, :, lanes] = jnp.where(front, a, pltpu.roll(b, PART, 1)).astype(BF)
-            nxt_out[2 * h + 1, :, lanes] = jnp.where(front, pltpu.roll(a, PART, 1), b).astype(BF)
-    pl.semaphore_wait(barrier, bands - 1)
+    told[...] = jnp.zeros(told.shape, jnp.int32)
+    told[:, 0:windows] = jnp.broadcast_to(keep_row[...], (8, windows))
+    mine = told[...]
+    rank = ranks(mine, windows)
+    final = jnp.max(jnp.where(iota(rank.shape, 1) == windows - 1, rank, 0.0), axis=1, keepdims=True)
+    line = iota(told.shape, 0)
+    extra = jnp.where(line == 1, jnp.broadcast_to(final, told.shape).astype(jnp.int32), live)
+    told[...] = jnp.where(line == 0, mine, extra)
 
     def nxt_copy(c):
         return pltpu.make_async_remote_copy(
@@ -246,7 +268,7 @@
         )
 
     odd = lax.rem(me, 2) == 1
-    fold = SHIFT // 2
+    fold = groups // 2
 
     def prv_send(part, source, start, device, mark):
         first = part * fold
@@ -260,8 +282,8 @@
         )
 
     direct = [prv_send(part, prv_out, 0, right, 0) for part in range(2)]
-    relay = [prv_send(part, prv_out, SHIFT, lax.rem(me + 2, bands), 1) for part in range(2)]
-    held = prv_buf.at[SHIFT:]
+    relay = [prv_send(part, prv_out, groups, lax.rem(me + 2, bands), 1) for part in range(2)]
+    held = prv_buf.at[groups:]
     forward = [prv_send(part, held, 0, left, 0) for part in range(2)]
     told_copy = pltpu.make_async_remote_copy(
         src_ref=told,
@@ -271,20 +293,35 @@
         device_id={"band": right},
         device_id_type=mesh_id,
     )
-    for c in range(groups):
-        nxt_copy(c).start()
-
-    for r in range(rows):
-        row = pltpu.roll(plane_row(planes, r, channels), cols - SHIFT, 1)
-        if r >= rows - SHIFT:
-            prv_out[r - rows + SHIFT] = row.astype(BF)
-        image[SHIFT + r] = row.T
+    pl.semaphore_wait(barrier, bands - 1)
+    told_copy.start()
+    moves[1].wait()
+    for h in range(halves):
+        part = pixels[:, :, h * LANES : (h + 1) * LANES].astype(F32)
+        planes[h] = part.reshape(channels * rows, LANES)
+
+    def arrange(first, matrix, target):
+        for r in range(0, SHIFT, 2):
+            one, two = (
+                dot(plane_row(planes, first + r + k, channels).astype(BF), matrix) for k in range(2)
+            )
+            lanes = slice(r * PART, (r + 2) * PART)
+            for h in range(halves):
+                cols_h = slice(h * LANES, (h + 1) * LANES)
+                even, uneven = swap_parts(one[:, cols_h], two[:, cols_h])
+                target[2 * h, :, lanes] = even.astype(BF)
+                target[2 * h + 1, :, lanes] = uneven.astype(BF)
+
+    columns[0] = column_order(rank, cols)
+    arrange(rows - SHIFT, columns[0], prv_out)
+
     @pl.when(odd)
     def _():
         for part in range(2):
             relay[part].start()
 
-    for move in moves[1:]:
+    order[...] = window_order()
+    for move in moves[2:]:
         move.wait()
     w_in[...] = dot_t(spread_heads(3 * DEPTH, 3 * CHAN), wqkv[...]).astype(BF)
     w_out[...] = dot(spread_heads(DEPTH, CHAN), wp[...]).T.astype(BF)
@@ -294,48 +331,24 @@
     bias_strips(table, strips)
     bias_fill(strips, bias, me == bands - 1, me == 0)
 
-    told[...] = jnp.zeros(told.shape, jnp.int32)
-    told[:, 0:windows] = jnp.broadcast_to(keep_row[...], (8, windows))
-    kept = told[...]
-    tri = (LANES, LANES)
-    before = lax.broadcasted_iota(jnp.int32, tri, 0) < lax.broadcasted_iota(jnp.int32, tri, 1)
-    place = dot(kept.astype(F32).astype(BF), jnp.where(before, 1.0, 0.0).astype(BF))
-    told[...] = jnp.where(place < count[0].astype(F32), kept, 0)
-
-    def spread(flags):
-        own_lane = (windows, LANES)
-        diagonal = lax.broadcasted_iota(jnp.int32, own_lane, 0) == lax.broadcasted_iota(
-            jnp.int32, own_lane, 1
-        )
-        chosen = jnp.where(diagonal, jnp.broadcast_to(flags[0:1].astype(F32), own_lane), 0.0)
-        return dot(chosen.astype(BF), jnp.ones((LANES, channels), BF))
-
-    told_copy.start()
-    active[0] = spread(told[...])
-
-    following[windows] = jnp.int32(windows)
-
-    def scan(i, kept_so_far):
-        w = windows - 1 - i
-        following[w] = jnp.where(keep[0, w] == 1, w, following[w + 1])
-        return kept_so_far + keep[0, w]
-
-    live = jnp.minimum(lax.fori_loop(0, windows, scan, jnp.int32(0)), count[0])
-
-    def rank(p, window):
-        order[p] = jnp.minimum(window, windows - 1)
-        return following[jnp.minimum(window + 1, windows)]
-
-    lax.fori_loop(0, windows, rank, following[0])
+    told_copy.wait()
+    news = told_buf[...]
+    columns[1] = column_order(ranks(jnp.broadcast_to(news[0:1], told.shape), windows), cols)
+    arrange(0, columns[1], nxt_out)
+    for c in range(groups):
+        nxt_copy(c).start()
+    live_prev, final_prev = news[2, 0], news[1, 0]
+    final_own = jnp.where(keep[0, windows - 1] == 1, live - 1, windows - 1)
 
     padded = channels + 4
-    early = iota((padded, LANES), 1) < TOK
-
-    def attend_windows(start, number, kind, row):
+
+    def windows_of(upper_part, lower_part):
+        return dot(jnp.concatenate([upper_part, lower_part], axis=1), order[...])
+
+    def attend_windows(x, start, kind, last):
         def edge(g):
-            return bias[2 * kind + (start + g == windows - 1).astype(jnp.int32)]
-
-        x = windows_at(image, start, number, row)
+            return bias[2 * kind + (start + g == last).astype(jnp.int32)]
+
         return attend(x, gains[0], w_in[...], w_out[...], edge)
 
     def step(c, _):
@@ -351,29 +364,17 @@
             for part in range(2):
                 direct[part].start()
 
-        block = nxt_buf[c].astype(F32).T
-        cut = pl.ds(pl.multiple_of(c * PART, PART), PART)
-        for r in range(SHIFT):
-            image[SHIFT + rows + r, cut, :] = block[r * PART : (r + 1) * PART]
-        own = attend_windows(c * GROUP, GROUP, 0, WIN)
+        x = windows_of(prv_out[c], nxt_buf[c])
+        origin[c] = x.astype(BF)
+        own = attend_windows(x, c * GROUP, 0, final_own)
         states[c] = own
         wide = jnp.concatenate([own.astype(F32), jnp.zeros((4, SIZE), F32)], axis=0)
-        for pair in range(GROUP // 2):
-            both = wide[:, pair * LANES : (pair + 1) * LANES]
-            turned = pltpu.roll(both, TOK, 1)
-            w = c * GROUP + 2 * pair
-            doubled[w] = jnp.where(early, both, turned).astype(BF)
-            doubled[w + 1] = jnp.where(early, turned, both).astype(BF)
+        for k in range(SIZE // LANES):
+            packed[c * (SIZE // LANES) + k] = wide[:, k * LANES : (k + 1) * LANES].astype(BF)
         return 0
 
-    lax.fori_loop(0, groups, step, 0)
-
-    @pl.when(odd)
-    def _():
-        relay[1].wait()
-        forward[1].start()
-
     slot_row = iota((padded, LANES), 0) >= channels
+    member = iota((padded, LANES), 1) // TOK
 
     def pack(index, peer, j):
         t = jnp.int32(0)
@@ -382,15 +383,10 @@
             hit = dests[0, j * span + i] == peer
             t = jnp.where(hit, j * span + i, t)
             found = jnp.where(hit, 1, found)
-        live_tile = (found > 0) & (t * TILE < live)
-        slot = jnp.where(live_tile, slots[0, t], CAP).astype(F32)
-        halves_of = []
-        for p in range(TILE):
-            position = t * TILE + p
-            valid = live_tile & (position < live)
-            value = doubled[order[position]]
-            halves_of.append(jnp.where(valid, value, jnp.zeros_like(value)))
-        value = jnp.where(early, halves_of[0], halves_of[1])
+        known = jnp.where(found > 0, live - t * TILE, 0)
+        slot = jnp.where(known > 0, slots[0, t], CAP).astype(F32)
+        value = packed[t]
+        value = jnp.where(member < known, value, jnp.zeros_like(value))
         outgoing[index] = jnp.where(slot_row, jnp.full((padded, LANES), slot, F32).astype(BF), value)
 
     def peer_of(n):
@@ -401,39 +397,39 @@
         side = lax.rem(lax.rem(me, 2) + cross, 2)
         return jnp.where(away, near, far) + 2 * row + side
 
-    def tile_copy(n):
+    def tile_copy(n, j):
         return pltpu.make_async_remote_copy(
-            src_ref=outgoing.at[pl.ds(n * pairs, pairs)],
-            dst_ref=incoming.at[pl.ds(me * pairs, pairs)],
-            send_sem=tile_send.at[n],
-            recv_sem=tile_recv.at[n],
+            src_ref=outgoing.at[n * pairs + j],
+            dst_ref=incoming.at[me * pairs + j],
+            send_sem=tile_send.at[n * pairs + j],
+            recv_sem=tile_recv.at[n * pairs + j],
             device_id={"band": peer_of(n)},
             device_id_type=mesh_id,
         )
 
-    def dispatch(n, _):
-        for j in range(pairs):
+    stage = groups // pairs
+
+    def round_of(j, _):
+        lax.fori_loop(j * stage, (j + 1) * stage, step, 0)
+
+        def dispatch(n, _):
             pack(n * pairs + j, peer_of(n), j)
-        tile_copy(n).start()
+            tile_copy(n, j).start()
+            return 0
+
+        lax.fori_loop(0, bands - 1, dispatch, 0)
+        kept_here = (bands - 1) * pairs + j
+        pack(kept_here, me, j)
+        incoming[me * pairs + j] = outgoing[kept_here]
         return 0
 
-    lax.fori_loop(0, bands - 1, dispatch, 0)
-    kept_here = (bands - 1) * pairs
-    for j in range(pairs):
-        pack(kept_here + j, me, j)
-    incoming[pl.ds(me * pairs, pairs)] = outgoing[kept_here : kept_here + pairs]
-
-    def blend(done, flags, w, row):
-        cols_w = pl.ds(pl.multiple_of(w * WIN, WIN), WIN)
-        chosen = active[flags, pl.ds(w, 1), :].reshape(1, 1, channels) > 0.5
-        result[row : row + SHIFT, cols_w, :] = jnp.where(
-            chosen,
-            done.reshape(SHIFT, WIN, CHAN),
-            image[SHIFT + row : 2 * SHIFT + row, cols_w, :],
-        )
-
-    told_copy.wait()
-    active[1] = spread(told_buf[...])
+    lax.fori_loop(0, pairs, round_of, 0)
+
+    @pl.when(odd)
+    def _():
+        relay[1].wait()
+        forward[1].start()
+
     for part in range(2):
         direct[part].wait_recv()
 
@@ -447,25 +443,34 @@
         for part in range(2):
             forward[part].wait_send()
 
-    for r in range(SHIFT):
-        image[r] = prv_buf[r].astype(F32).T
-    upper = iota((channels, WIDER * SIZE), 1) % TOK < HALF
+    lane = iota((channels, WIDER * SIZE), 1)
+    upper = lane % TOK < HALF
 
     def finish(i, _):
         number = WIDER * GROUP
-        prev = attend_windows(i * number, number, 1, 0)
-        own = jnp.concatenate([states[i * WIDER + k] for k in range(WIDER)], axis=1)
-        mine = jnp.where(upper, own, prev)
-        done = feed(mine, gains[1], w_hid[...], wo[...]).astype(F32).T
-        for g in range(number):
-            w = i * number + g
-            blend(done[g * TOK : g * TOK + HALF], 0, w, SHIFT)
-            blend(done[g * TOK + HALF : (g + 1) * TOK], 1, w, 0)
+        chunks = [i * WIDER + k for k in range(WIDER)]
+        x = jnp.concatenate([windows_of(prv_buf[c], nxt_out[c]) for c in chunks], axis=1)
+        prev = attend_windows(x, i * number, 1, final_prev)
+        own = jnp.concatenate([states[c] for c in chunks], axis=1)
+        done = feed(jnp.where(upper, own, prev), gains[1], w_hid[...], wo[...])
+        before = jnp.concatenate([origin[c] for c in chunks], axis=1)
+        before = jnp.where(upper, before, x.astype(BF))
+        position = i * number + lane // TOK
+        chosen = position < jnp.where(upper, live, live_prev)
+        after = jnp.where(chosen, done, before)
+        one, two = (dot_t(after[:, k * SIZE : (k + 1) * SIZE], order[...]) for k in range(WIDER))
+        for k in range(SIZE // LANES):
+            cut = slice(k * LANES, (k + 1) * LANES)
+            even, uneven = swap_parts(one[:, cut], two[:, cut])
+            r = (2 * k + SHIFT) % rows
+            done_rows[i, r] = even.astype(BF)
+            done_rows[i, r + 1] = uneven.astype(BF)
         return 0
 
     lax.fori_loop(0, groups // WIDER, finish, 0)
     for r in range(rows):
-        row = pltpu.roll(result[r].T, SHIFT, 1)
+        row = jnp.concatenate([done_rows[h, r] for h in range(halves)], axis=1)
+        row = dot_t(row, columns[0] if r >= rows - SHIFT else columns[1])
         for h in range(halves):
             planes[h, pl.ds(r, channels, stride=WIN), :] = row[:, h * LANES : (h + 1) * LANES]
     for h in range(halves):
@@ -474,7 +479,8 @@
         )
 
     def collect(i, _):
-        tile_copy(i).wait()
+        for j in range(pairs):
+            tile_copy(i, j).wait()
         return 0
 
     lax.fori_loop(0, bands - 1, collect, 0)
@@ -535,11 +541,10 @@
             *(pltpu.VMEM(operand.shape, operand.dtype) for operand in operands[3:]),
             pltpu.SemaphoreType.DMA((len(operands) + 1,)),
             pltpu.VMEM((halves, channels * rows, LANES), F32),
-            pltpu.VMEM((rows + 2 * SHIFT, cols, channels), F32),
             pltpu.VMEM(nxt_shape, BF),
-            pltpu.VMEM((SHIFT, channels, cols), BF),
             pltpu.VMEM(nxt_shape, BF),
-            pltpu.VMEM((2 * SHIFT, channels, cols), BF),
+            pltpu.VMEM(nxt_shape, BF),
+            pltpu.VMEM((2 * groups, channels, SHIFT * PART), BF),
             pltpu.VMEM((8, LANES), jnp.int32),
             pltpu.VMEM((8, LANES), jnp.int32),
             pltpu.VMEM((3 * DEPTH, channels), BF),
@@ -548,17 +553,17 @@
             pltpu.VMEM((2, channels, LANES), F32),
             pltpu.VMEM((8 * WIN, LANES), F32),
             pltpu.VMEM((4, TOK, QUERIES), F32),
+            pltpu.VMEM((SIZE, SIZE), BF),
+            pltpu.VMEM((2, cols, cols), BF),
             pltpu.VMEM((groups, channels, SIZE), BF),
-            pltpu.VMEM((windows, channels + 4, LANES), BF),
-            pltpu.VMEM((rows, cols, channels), F32),
-            pltpu.VMEM((2, windows, channels), F32),
+            pltpu.VMEM((groups, channels, SIZE), BF),
+            pltpu.VMEM((halves, rows, channels, LANES), BF),
+            pltpu.VMEM((tiles, channels + 4, LANES), BF),
             pltpu.VMEM(tile_shape, BF),
-            pltpu.SMEM((windows + 1,), jnp.int32),
-            pltpu.SMEM((windows,), jnp.int32),
             pltpu.SemaphoreType.DMA((groups + 5,)),
             pltpu.SemaphoreType.DMA((groups + 5,)),
-            pltpu.SemaphoreType.DMA((bands,)),
-            pltpu.SemaphoreType.DMA((bands,)),
+            pltpu.SemaphoreType.DMA((bands * pairs,)),
+            pltpu.SemaphoreType.DMA((bands * pairs,)),
         ],
         compiler_params=pltpu.CompilerParams(
             vmem_limit_bytes=40 * 1024 * 1024, collective_id=0, has_side_effects=True

time: 42.2 us -> 47.5 us (1.13)
  Pallas kernels: 40.7 us -> 46.1 us
    pallas_call x1, Pallas kernels: 38.8 us -> 44.1 us  [shards(): pl.pallas_call(block_kernel, out_shape=(jax.ShapeDtypeStruct((channels, r...]
where the time goes in v5:
time: 47.5 us; the launch traced here: 47.3 us
  Pallas kernels  46.1 us (97%)
  between operations  1.29 us (3%)
    pallas_call x1, Pallas kernels, shards(): pl.pallas_call(block_kernel, out_shape=(jax.ShapeDtypeStruct((channels, r...  44.1 us
    pallas_call x1, Pallas kernels, shards(): pl.pallas_call(place_kernel, out_shape=(jax.ShapeDtypeStruct((channels, r...  1.9 us

profile of v5, /device:TPU:0, one launch (start us, length us, event | category | flops | bytes accessed | tf_op | source)
XLA Modules:
  0.0 47.3 jit_solution(12638730163126788941)
XLA Ops:
  1.3 44.1 %block.1 = (bf16[180,8,256]{2,1,0:T(8,128)(2,1)S(1)}, bf16[16,184,128]{2,1,0:T(8,128)(2,1)S(1)}) custom-call(s32[1]{0:T(128)S(6)} %copy.14.count, s32[1,32]{1,0:T(1,128)} %keep_in.1, s32[1,16]{1,0:T(1,128)} %dests_in.1, s32[1,16]{1,0:T(1,128)} %slots_in.1, bf16[180,8,256]{2,1,0:T(8,128)(2,1)} %bitcast.7, f32[6,225]{1,0:T(8,128)} %bitcast.11, ...), custom_call_target="tpu_custom_call" | custom-call | flops 10000000000 | bytes 10000000 | tf_op jit(solution)/shard_map/block/pallas_call | solution.py:528
  45.4 1.9 %place.1 = (bf16[180,8,256]{2,1,0:T(8,128)(2,1)}, bf16[180,8,128]{2,1,0:T(8,128)(2,1)}) custom-call(bf16[16,184,128]{2,1,0:T(8,128)(2,1)S(1)} %get-tuple-element.6.incoming, bf16[180,8,256]{2,1,0:T(8,128)(2,1)S(1)} %get-tuple-element.7.restored), custom_call_target="tpu_custom_call" | custom-call | tf_op jit(solution)/shard_map/place/pallas_call | solution.py:574

commit v6 on v5

--- a/solution.py
+++ b/solution.py
@@ -17,6 +17,7 @@
 GROUP = 8
 WIDER = 2
 SIZE = GROUP * TOK
+AHEAD = 4
 PART = GROUP * WIN
 PAD = 32
 DEPTH = HEADS * PAD
@@ -109,8 +110,9 @@
     v = mixed[2 * DEPTH :].astype(BF)
     low = iota((PAD, LANES), 1) < TOK
     blank = jnp.zeros((PAD, LANES), F32)
-    joined = []
-    for pair in range(x.shape[1] // LANES):
+    none = jnp.zeros((TOK, LANES), BF)
+
+    def weigh(pair):
         lanes = slice(pair * LANES, (pair + 1) * LANES)
         q_pair = q[:, lanes]
         q_turn = pltpu.roll(q_pair, TOK, 1)
@@ -130,8 +132,11 @@
             top = jnp.max(scores, axis=0, keepdims=True)
             grown = jnp.exp(scores - top)
             weights.append((grown * (1.0 / jnp.sum(grown, axis=0, keepdims=True))).astype(BF))
+        return weights
+
+    def mix(pair, weights):
+        lanes = slice(pair * LANES, (pair + 1) * LANES)
         rows = []
-        none = jnp.zeros((TOK, LANES), BF)
         for j in range(HEADS // 2):
             cut = slice(j * LANES, (j + 1) * LANES)
             both = jnp.concatenate(
@@ -145,8 +150,16 @@
             one, two = found[:, :LANES], found[:, LANES:]
             rows.append(jnp.where(low, one[:PAD], pltpu.roll(two[:PAD], TOK, 1)))
             rows.append(jnp.where(low, pltpu.roll(one[PAD:], TOK, 1), two[PAD:]))
-        joined.append(jnp.concatenate(rows, axis=0))
-    joined = jnp.concatenate(joined, axis=1).astype(BF)
+        return jnp.concatenate(rows, axis=0).astype(BF)
+
+    count = x.shape[1] // LANES
+    ready, joined = {}, []
+    for pair in range(count + AHEAD):
+        if pair < count:
+            ready[pair] = weigh(pair)
+        if pair >= AHEAD:
+            joined.append(mix(pair - AHEAD, ready.pop(pair - AHEAD)))
+    joined = jnp.concatenate(joined, axis=1)
     return (x + dot(w_out, joined)).astype(BF)
 
 
@@ -228,9 +241,9 @@
         pltpu.make_async_copy(source, target, loads.at[i])
         for i, (source, target) in enumerate(
             (
-                (keep_in, keep_row), (pixels_in, pixels), (wqkv_in, wqkv), (wp_in, wp),
+                (keep_in, keep_row), (pixels_in, pixels), (keep_in, keep), (wqkv_in, wqkv), (wp_in, wp),
                 (table_in, table), (gain_a_in, gain_a), (gain_m_in, gain_m), (wh_in, wh),
-                (wo_in, wo), (keep_in, keep), (dests_in, dests), (slots_in, slots),
+                (wo_in, wo), (dests_in, dests), (slots_in, slots),
             )
         )
     ]
@@ -255,7 +268,7 @@
     final = jnp.max(jnp.where(iota(rank.shape, 1) == windows - 1, rank, 0.0), axis=1, keepdims=True)
     line = iota(told.shape, 0)
     extra = jnp.where(line == 1, jnp.broadcast_to(final, told.shape).astype(jnp.int32), live)
-    told[...] = jnp.where(line == 0, mine, extra)
+    told[...] = jnp.where(line == 0, rank.astype(jnp.int32), extra)
 
     def nxt_copy(c):
         return pltpu.make_async_remote_copy(
@@ -268,23 +281,28 @@
         )
 
     odd = lax.rem(me, 2) == 1
-    fold = groups // 2
-
-    def prv_send(part, source, start, device, mark):
+    fold = WIDER
+
+    def prv_send(part, source, from_chunk, to_chunk, device, mark):
         first = part * fold
         return pltpu.make_async_remote_copy(
-            src_ref=source.at[first : first + fold],
-            dst_ref=prv_buf.at[start + first : start + first + fold],
+            src_ref=source.at[pl.ds(from_chunk + first, fold)],
+            dst_ref=prv_buf.at[pl.ds(to_chunk + first, fold)],
             send_sem=halo_send.at[groups + 1 + 2 * mark + part],
             recv_sem=halo_recv.at[groups + 1 + 2 * mark + part],
             device_id={"band": device},
             device_id_type=mesh_id,
         )
 
-    direct = [prv_send(part, prv_out, 0, right, 0) for part in range(2)]
-    relay = [prv_send(part, prv_out, groups, lax.rem(me + 2, bands), 1) for part in range(2)]
-    held = prv_buf.at[groups:]
-    forward = [prv_send(part, held, 0, left, 0) for part in range(2)]
+    def direct(part):
+        return prv_send(part, prv_out, 0, 0, right, 0)
+
+    def relay(part):
+        return prv_send(part, prv_out, 0, groups, lax.rem(me + 2, bands), 1)
+
+    def forward(part):
+        return prv_send(part, prv_buf, groups, 0, left, 0)
+
     told_copy = pltpu.make_async_remote_copy(
         src_ref=told,
         dst_ref=told_buf,
@@ -296,32 +314,45 @@
     pl.semaphore_wait(barrier, bands - 1)
     told_copy.start()
     moves[1].wait()
+    moves[2].wait()
     for h in range(halves):
         part = pixels[:, :, h * LANES : (h + 1) * LANES].astype(F32)
         planes[h] = part.reshape(channels * rows, LANES)
 
-    def arrange(first, matrix, target):
-        for r in range(0, SHIFT, 2):
-            one, two = (
-                dot(plane_row(planes, first + r + k, channels).astype(BF), matrix) for k in range(2)
-            )
-            lanes = slice(r * PART, (r + 2) * PART)
-            for h in range(halves):
-                cols_h = slice(h * LANES, (h + 1) * LANES)
-                even, uneven = swap_parts(one[:, cols_h], two[:, cols_h])
+    def arrange(first, matrix, target, done):
+        moved = [
+            dot(plane_row(planes, first + r, channels).astype(BF), matrix) for r in range(SHIFT)
+        ]
+        for h in range(halves):
+            cols_h = slice(h * LANES, (h + 1) * LANES)
+            for r in range(0, SHIFT, 2):
+                even, uneven = swap_parts(moved[r][:, cols_h], moved[r + 1][:, cols_h])
+                lanes = slice(r * PART, (r + 2) * PART)
                 target[2 * h, :, lanes] = even.astype(BF)
                 target[2 * h + 1, :, lanes] = uneven.astype(BF)
+            done(h)
 
     columns[0] = column_order(rank, cols)
-    arrange(rows - SHIFT, columns[0], prv_out)
-
-    @pl.when(odd)
-    def _():
-        for part in range(2):
-            relay[part].start()
+
+    def start_relay(h):
+        @pl.when(odd)
+        def _():
+            relay(h).start()
+
+    def start_nxt(h):
+        nxt_copy(2 * h).start()
+        nxt_copy(2 * h + 1).start()
+
+    arrange(rows - SHIFT, columns[0], prv_out, start_relay)
+    told_copy.wait()
+    news = told_buf[...]
+    columns[1] = column_order(news[0:1].astype(F32), cols)
+    arrange(0, columns[1], nxt_out, start_nxt)
+    live_prev, final_prev = news[2, 0], news[1, 0]
+    final_own = jnp.where(keep[0, windows - 1] == 1, live - 1, windows - 1)
 
     order[...] = window_order()
-    for move in moves[2:]:
+    for move in moves[3:]:
         move.wait()
     w_in[...] = dot_t(spread_heads(3 * DEPTH, 3 * CHAN), wqkv[...]).astype(BF)
     w_out[...] = dot(spread_heads(DEPTH, CHAN), wp[...]).T.astype(BF)
@@ -331,15 +362,6 @@
     bias_strips(table, strips)
     bias_fill(strips, bias, me == bands - 1, me == 0)
 
-    told_copy.wait()
-    news = told_buf[...]
-    columns[1] = column_order(ranks(jnp.broadcast_to(news[0:1], told.shape), windows), cols)
-    arrange(0, columns[1], nxt_out)
-    for c in range(groups):
-        nxt_copy(c).start()
-    live_prev, final_prev = news[2, 0], news[1, 0]
-    final_own = jnp.where(keep[0, windows - 1] == 1, live - 1, windows - 1)
-
     padded = channels + 4
 
     def windows_of(upper_part, lower_part):
@@ -354,15 +376,15 @@
     def step(c, _):
         nxt_copy(c).wait()
 
-        @pl.when((c == groups - 1) & odd)
+        @pl.when((c >= groups - 2) & odd)
         def _():
-            relay[0].wait()
-            forward[0].start()
+            relay(c - groups + 2).wait()
+            forward(c - groups + 2).start()
 
         @pl.when((c == groups - 1) & ~odd)
         def _():
-            for part in range(2):
-                direct[part].start()
+            direct(0).start()
+            direct(1).start()
 
         x = windows_of(prv_out[c], nxt_buf[c])
         origin[c] = x.astype(BF)
@@ -425,28 +447,20 @@
 
     lax.fori_loop(0, pairs, round_of, 0)
 
-    @pl.when(odd)
-    def _():
-        relay[1].wait()
-        forward[1].start()
-
-    for part in range(2):
-        direct[part].wait_recv()
-
-    @pl.when(~odd)
-    def _():
-        for part in range(2):
-            direct[part].wait_send()
-
-    @pl.when(odd)
-    def _():
-        for part in range(2):
-            forward[part].wait_send()
-
     lane = iota((channels, WIDER * SIZE), 1)
     upper = lane % TOK < HALF
 
     def finish(i, _):
+        direct(i).wait_recv()
+
+        @pl.when(~odd)
+        def _():
+            direct(i).wait_send()
+
+        @pl.when(odd)
+        def _():
+            forward(i).wait_send()
+
         number = WIDER * GROUP
         chunks = [i * WIDER + k for k in range(WIDER)]
         x = jnp.concatenate([windows_of(prv_buf[c], nxt_out[c]) for c in chunks], axis=1)

time: 47.5 us -> 41.1 us (0.87)
  Pallas kernels: 46.1 us -> 39.7 us
    pallas_call x1, Pallas kernels: 44.1 us -> 37.8 us  [shards(): pl.pallas_call(block_kernel, out_shape=(jax.ShapeDtypeStruct((channels, r...]
where the time goes in v6:
time: 41.1 us; the launch traced here: 40.9 us
  Pallas kernels  39.7 us (97%)
  between operations  1.29 us (3%)
    pallas_call x1, Pallas kernels, shards(): pl.pallas_call(block_kernel, out_shape=(jax.ShapeDtypeStruct((channels, r...  37.8 us
    pallas_call x1, Pallas kernels, shards(): pl.pallas_call(place_kernel, out_shape=(jax.ShapeDtypeStruct((channels, r...  1.9 us

profile of v6, /device:TPU:0, one launch (start us, length us, event | category | flops | bytes accessed | tf_op | source)
XLA Modules:
  0.0 40.9 jit_solution(18434779133539811035)
XLA Ops:
  1.3 37.8 %block.1 = (bf16[180,8,256]{2,1,0:T(8,128)(2,1)S(1)}, bf16[16,184,128]{2,1,0:T(8,128)(2,1)S(1)}) custom-call(s32[1]{0:T(128)S(6)} %copy.14.count, s32[1,32]{1,0:T(1,128)} %keep_in.1, s32[1,16]{1,0:T(1,128)} %dests_in.1, s32[1,16]{1,0:T(1,128)} %slots_in.1, bf16[180,8,256]{2,1,0:T(8,128)(2,1)} %bitcast.7, f32[6,225]{1,0:T(8,128)} %bitcast.11, ...), custom_call_target="tpu_custom_call" | custom-call | flops 10000000000 | bytes 10000000 | tf_op jit(solution)/shard_map/block/pallas_call | solution.py:542
  39.0 1.9 %place.1 = (bf16[180,8,256]{2,1,0:T(8,128)(2,1)}, bf16[180,8,128]{2,1,0:T(8,128)(2,1)}) custom-call(bf16[16,184,128]{2,1,0:T(8,128)(2,1)S(1)} %get-tuple-element.6.incoming, bf16[180,8,256]{2,1,0:T(8,128)(2,1)S(1)} %get-tuple-element.7.restored), custom_call_target="tpu_custom_call" | custom-call | tf_op jit(solution)/shard_map/place/pallas_call | solution.py:588

commit v7 on v6

--- a/solution.py
+++ b/solution.py
@@ -18,6 +18,7 @@
 WIDER = 2
 SIZE = GROUP * TOK
 AHEAD = 4
+CUT = 60
 PART = GROUP * WIN
 PAD = 32
 DEPTH = HEADS * PAD
@@ -335,9 +336,13 @@
     columns[0] = column_order(rank, cols)
 
     def start_relay(h):
+        if h == 0:
+            direct(0).start()
+            return
+
         @pl.when(odd)
         def _():
-            relay(h).start()
+            relay(1).start()
 
     def start_nxt(h):
         nxt_copy(2 * h).start()
@@ -376,14 +381,13 @@
     def step(c, _):
         nxt_copy(c).wait()
 
-        @pl.when((c >= groups - 2) & odd)
+        @pl.when((c == 1) & odd)
         def _():
-            relay(c - groups + 2).wait()
-            forward(c - groups + 2).start()
+            relay(1).wait()
+            forward(1).start()
 
         @pl.when((c == groups - 1) & ~odd)
         def _():
-            direct(0).start()
             direct(1).start()
 
         x = windows_of(prv_out[c], nxt_buf[c])
@@ -453,11 +457,11 @@
     def finish(i, _):
         direct(i).wait_recv()
 
-        @pl.when(~odd)
+        @pl.when(~odd | (i == 0))
         def _():
             direct(i).wait_send()
 
-        @pl.when(odd)
+        @pl.when(odd & (i > 0))
         def _():
             forward(i).wait_send()
 
@@ -500,23 +504,41 @@
     lax.fori_loop(0, bands - 1, collect, 0)
 
 
-def place_kernel(incoming, restored, restored_out, work, planes, sem):
+def place_kernel(incoming, restored, restored_out, work_out, planes, work, sems):
     total, padded, _ = incoming.shape
     channels = work.shape[0]
-    move = pltpu.make_async_copy(restored, restored_out, sem)
-    move.start()
+    blocks = range(0, channels, CUT)
+    moves = [
+        pltpu.make_async_copy(restored.at[b : b + CUT], restored_out.at[b : b + CUT], sems.at[0, i])
+        for i, b in enumerate(blocks)
+    ]
+    for move in moves:
+        move.start()
     head = incoming[:, padded - 8 :, :].astype(F32)
     head = jnp.max(jnp.where(iota(head.shape, 1) >= 4, head, 0.0), axis=1)
     slot = jnp.max(head, axis=1, keepdims=True).astype(jnp.int32)
     match = slot == iota((total, LANES), 1)
     source = jnp.where(match, iota((total, LANES), 0), -1).astype(F32)
     source = jnp.max(source, axis=0, keepdims=True).astype(jnp.int32)
-    for k in range(CAP):
-        known = source[0, k] >= 0
-        block = incoming[jnp.maximum(source[0, k], 0)].astype(F32)[:channels]
-        planes[pl.ds(k, channels, stride=CAP), :] = jnp.where(known, block, 0.0)
-    work[...] = planes[...].reshape(channels, CAP, TILE * TOK).astype(BF)
-    move.wait()
+    chosen = [source[0, k] for k in range(CAP)]
+    sent = []
+    for i, b in enumerate(blocks):
+        for k in range(CAP):
+            block = incoming[jnp.maximum(chosen[k], 0), b : b + CUT].astype(F32)
+            block = jnp.where(chosen[k] >= 0, block, 0.0)
+            planes[pl.ds(b * CAP + k, CUT, stride=CAP), :] = block
+        value = planes[b * CAP : (b + CUT) * CAP].reshape(CUT, CAP, TILE * TOK)
+        work[b : b + CUT] = value.astype(BF)
+        sent.append(
+            pltpu.make_async_copy(work.at[b : b + CUT], work_out.at[b : b + CUT], sems.at[1, i])
+        )
+        if i > 0:
+            sent[i - 1].start()
+    for move in moves:
+        move.wait()
+    sent[-1].start()
+    for move in sent:
+        move.wait()
 
 
 def shards(
@@ -592,10 +614,11 @@
             jax.ShapeDtypeStruct((channels, CAP, TILE * TOK), BF),
         ),
         in_specs=[vmem, vmem],
-        out_specs=(pl.BlockSpec(memory_space=pl.ANY), vmem),
+        out_specs=(pl.BlockSpec(memory_space=pl.ANY), pl.BlockSpec(memory_space=pl.ANY)),
         scratch_shapes=[
             pltpu.VMEM((channels * CAP, TILE * TOK), F32),
-            pltpu.SemaphoreType.DMA,
+            pltpu.VMEM((channels, CAP, TILE * TOK), BF),
+            pltpu.SemaphoreType.DMA((2, -(-channels // CUT))),
         ],
         compiler_params=pltpu.CompilerParams(vmem_limit_bytes=16 * 1024 * 1024),
         name="place",

time: 41.1 us -> 37.8 us (0.920)
  Pallas kernels: 39.7 us -> 36.3 us
    pallas_call x1, Pallas kernels: 37.8 us -> 34.5 us  [shards(): pl.pallas_call(block_kernel, out_shape=(jax.ShapeDtypeStruct((channels, r...]
where the time goes in v7:
time: 37.8 us; the launch traced here: 37.6 us
  Pallas kernels  36.3 us (96%)
  between operations  1.29 us (3%)
    pallas_call x1, Pallas kernels, shards(): pl.pallas_call(block_kernel, out_shape=(jax.ShapeDtypeStruct((channels, r...  34.5 us
    pallas_call x1, Pallas kernels, shards(): pl.pallas_call(place_kernel, out_shape=(jax.ShapeDtypeStruct((channels, r...  1.77 us

profile of v7, /device:TPU:0, one launch (start us, length us, event | category | flops | bytes accessed | tf_op | source)
XLA Modules:
  0.0 37.6 jit_solution(8184997269896996226)
XLA Ops:
  1.3 34.5 %block.1 = (bf16[180,8,256]{2,1,0:T(8,128)(2,1)S(1)}, bf16[16,184,128]{2,1,0:T(8,128)(2,1)S(1)}) custom-call(s32[1]{0:T(128)S(6)} %copy.14.count, s32[1,32]{1,0:T(1,128)} %keep_in.1, s32[1,16]{1,0:T(1,128)} %dests_in.1, s32[1,16]{1,0:T(1,128)} %slots_in.1, bf16[180,8,256]{2,1,0:T(8,128)(2,1)} %bitcast.7, f32[6,225]{1,0:T(8,128)} %bitcast.11, ...), custom_call_target="tpu_custom_call" | custom-call | flops 10000000000 | bytes 10000000 | tf_op jit(solution)/shard_map/block/pallas_call | solution.py:564
  35.8 1.8 %place.1 = (bf16[180,8,256]{2,1,0:T(8,128)(2,1)}, bf16[180,8,128]{2,1,0:T(8,128)(2,1)}) custom-call(bf16[16,184,128]{2,1,0:T(8,128)(2,1)S(1)} %get-tuple-element.6.incoming, bf16[180,8,256]{2,1,0:T(8,128)(2,1)S(1)} %get-tuple-element.7.restored), custom_call_target="tpu_custom_call" | custom-call | tf_op jit(solution)/shard_map/place/pallas_call | solution.py:610

commit v8 on v7

--- a/solution.py
+++ b/solution.py
@@ -266,10 +266,8 @@
     told[:, 0:windows] = jnp.broadcast_to(keep_row[...], (8, windows))
     mine = told[...]
     rank = ranks(mine, windows)
-    final = jnp.max(jnp.where(iota(rank.shape, 1) == windows - 1, rank, 0.0), axis=1, keepdims=True)
     line = iota(told.shape, 0)
-    extra = jnp.where(line == 1, jnp.broadcast_to(final, told.shape).astype(jnp.int32), live)
-    told[...] = jnp.where(line == 0, rank.astype(jnp.int32), extra)
+    told[...] = jnp.where(line == 0, rank.astype(jnp.int32), live)
 
     def nxt_copy(c):
         return pltpu.make_async_remote_copy(
@@ -353,7 +351,7 @@
     news = told_buf[...]
     columns[1] = column_order(news[0:1].astype(F32), cols)
     arrange(0, columns[1], nxt_out, start_nxt)
-    live_prev, final_prev = news[2, 0], news[1, 0]
+    live_prev, final_prev = news[1, 0], news[0, windows - 1]
     final_own = jnp.where(keep[0, windows - 1] == 1, live - 1, windows - 1)
 
     order[...] = window_order()
@@ -532,11 +530,9 @@
         sent.append(
             pltpu.make_async_copy(work.at[b : b + CUT], work_out.at[b : b + CUT], sems.at[1, i])
         )
-        if i > 0:
-            sent[i - 1].start()
+        sent[-1].start()
     for move in moves:
         move.wait()
-    sent[-1].start()
     for move in sent:
         move.wait()
 

time: 37.8 us -> 37.3 us (0.987)
  Pallas kernels: 36.3 us -> 35.8 us
    pallas_call x1, Pallas kernels: 1.77 us -> 1.31 us  [shards(): pl.pallas_call(place_kernel, out_shape=(jax.ShapeDtypeStruct((channels, r...]
where the time goes in v8:
time: 37.3 us; the launch traced here: 37.1 us
  Pallas kernels  35.8 us (96%)
  between operations  1.29 us (3%)
    pallas_call x1, Pallas kernels, shards(): pl.pallas_call(block_kernel, out_shape=(jax.ShapeDtypeStruct((channels, r...  34.5 us
    pallas_call x1, Pallas kernels, shards(): pl.pallas_call(place_kernel, out_shape=(jax.ShapeDtypeStruct((channels, r...  1.31 us

profile of v8, /device:TPU:0, one launch (start us, length us, event | category | flops | bytes accessed | tf_op | source)
XLA Modules:
  0.0 37.1 jit_solution(146701555279327737)
XLA Ops:
  1.3 34.5 %block.1 = (bf16[180,8,256]{2,1,0:T(8,128)(2,1)S(1)}, bf16[16,184,128]{2,1,0:T(8,128)(2,1)S(1)}) custom-call(s32[1]{0:T(128)S(6)} %copy.14.count, s32[1,32]{1,0:T(1,128)} %keep_in.1, s32[1,16]{1,0:T(1,128)} %dests_in.1, s32[1,16]{1,0:T(1,128)} %slots_in.1, bf16[180,8,256]{2,1,0:T(8,128)(2,1)} %bitcast.7, f32[6,225]{1,0:T(8,128)} %bitcast.11, ...), custom_call_target="tpu_custom_call" | custom-call | flops 10000000000 | bytes 10000000 | tf_op jit(solution)/shard_map/block/pallas_call | solution.py:560
  35.8 1.3 %place.1 = (bf16[180,8,256]{2,1,0:T(8,128)(2,1)}, bf16[180,8,128]{2,1,0:T(8,128)(2,1)}) custom-call(bf16[16,184,128]{2,1,0:T(8,128)(2,1)S(1)} %get-tuple-element.6.incoming, bf16[180,8,256]{2,1,0:T(8,128)(2,1)S(1)} %get-tuple-element.7.restored), custom_call_target="tpu_custom_call" | custom-call | tf_op jit(solution)/shard_map/place/pallas_call | solution.py:606

commit v9 on v8

--- a/solution.py
+++ b/solution.py
@@ -329,6 +329,7 @@
                 lanes = slice(r * PART, (r + 2) * PART)
                 target[2 * h, :, lanes] = even.astype(BF)
                 target[2 * h + 1, :, lanes] = uneven.astype(BF)
+        for h in range(halves):
             done(h)
 
     columns[0] = column_order(rank, cols)
@@ -438,12 +439,17 @@
 
         def dispatch(n, _):
             pack(n * pairs + j, peer_of(n), j)
-            tile_copy(n, j).start()
+
+            @pl.when(n > 0)
+            def _():
+                tile_copy(n - 1, j).start()
+
             return 0
 
         lax.fori_loop(0, bands - 1, dispatch, 0)
         kept_here = (bands - 1) * pairs + j
         pack(kept_here, me, j)
+        tile_copy(bands - 2, j).start()
         incoming[me * pairs + j] = outgoing[kept_here]
         return 0
 

time: 37.3 us -> 37.4 us (level)
  no operation moved by 1% of the time
where the time goes in v9:
time: 37.4 us; the launch traced here: 37.2 us
  Pallas kernels  35.9 us (96%)
  between operations  1.29 us (3%)
    pallas_call x1, Pallas kernels, shards(): pl.pallas_call(block_kernel, out_shape=(jax.ShapeDtypeStruct((channels, r...  34.6 us
    pallas_call x1, Pallas kernels, shards(): pl.pallas_call(place_kernel, out_shape=(jax.ShapeDtypeStruct((channels, r...  1.31 us

profile of v9, /device:TPU:0, one launch (start us, length us, event | category | flops | bytes accessed | tf_op | source)
XLA Modules:
  0.0 37.2 jit_solution(4112605625356926880)
XLA Ops:
  1.3 34.6 %block.1 = (bf16[180,8,256]{2,1,0:T(8,128)(2,1)S(1)}, bf16[16,184,128]{2,1,0:T(8,128)(2,1)S(1)}) custom-call(s32[1]{0:T(128)S(6)} %copy.14.count, s32[1,32]{1,0:T(1,128)} %keep_in.1, s32[1,16]{1,0:T(1,128)} %dests_in.1, s32[1,16]{1,0:T(1,128)} %slots_in.1, bf16[180,8,256]{2,1,0:T(8,128)(2,1)} %bitcast.7, f32[6,225]{1,0:T(8,128)} %bitcast.11, ...), custom_call_target="tpu_custom_call" | custom-call | flops 10000000000 | bytes 10000000 | tf_op jit(solution)/shard_map/block/pallas_call | solution.py:566
  35.9 1.3 %place.1 = (bf16[180,8,256]{2,1,0:T(8,128)(2,1)}, bf16[180,8,128]{2,1,0:T(8,128)(2,1)}) custom-call(bf16[16,184,128]{2,1,0:T(8,128)(2,1)S(1)} %get-tuple-element.6.incoming, bf16[180,8,256]{2,1,0:T(8,128)(2,1)S(1)} %get-tuple-element.7.restored), custom_call_target="tpu_custom_call" | custom-call | tf_op jit(solution)/shard_map/place/pallas_call | solution.py:612
